TPU v7x, 256 devices: a whole 4x4x8 slice. The times are simulated.
256 devices in a mesh: seq: 32 (over z, x), batch: 8 (over y, core).
Axes of the slice: x: 4, y: 4, z: 8, core: 2. Of those that a mesh axis runs over, the one named last changes fastest.
Arguments:
- inputs: bfloat16 [8, 8192, 6144], P('batch', 'seq'), may hold values from -6 to 6
- out_grad: bfloat16 [8, 8192, 6144], P('batch', 'seq'), may hold values from -6 to 6
- step_size: float32 [8, 96, 8192], P('batch', None, 'seq'), may hold values from 0.5 to 2
- log_decay: float32 [8, 96, 8192], P('batch', None, 'seq'), may hold values from -1 to 0
- b_matrix: bfloat16 [8, 16, 8192], P('batch', None, 'seq'), may hold values from -1.5 to 1.5
- c_matrix: bfloat16 [8, 16, 8192], P('batch', None, 'seq'), may hold values from -0.0625 to 0.0625
- skip_gain: float32 [96], replicated, may hold values from 0.5 to 1.5
- lengths: int32 [8], P('batch'), may hold values from 256 to 8192
Outputs:
- grad_x: bfloat16 [8, 8192, 6144], P('batch', 'seq')
- grad_b: float32 [8, 16, 8192], P('batch', None, 'seq')
- grad_c: float32 [8, 16, 8192], P('batch', None, 'seq')
All inputs are finite; a program needn't handle non-finite values.
Results may differ from a plain program's by a relative error of at most 0.0047.
Values may be sent and summed in bfloat16 or wider, within the bound.
A program may use at most 128 MiB of HBM per device.

v0:
```python
import math

import jax
import jax.numpy as jnp
from jax import lax
from jax.sharding import Mesh
from jax.sharding import PartitionSpec as P

SPAN = 256
SEQ = ("seq_0", "seq_1")


HIGHEST = lax.Precision.HIGHEST


def neutral_like(shard, identity):
    return jax.tree.map(
        lambda part, zero: jnp.zeros_like(part) + jnp.asarray(zero, part.dtype), shard, identity
    )


def entering(shard, axes, combine, identity, reverse):
    before = start = neutral_like(shard, identity)
    so_far = shard
    for axis in reversed(axes):
        peers, position = (lax.axis_size(axis), lax.axis_index(axis))
        pieces = jax.tree.map(lambda part: lax.all_gather(part, axis), so_far)
        inside, so_far = (start, start)
        for k in reversed(range(peers)) if reverse else range(peers):
            passed = k > position if reverse else k < position
            so_far = combine(so_far, jax.tree.map(lambda part: part[k], pieces))
            inside = jax.tree.map(lambda new, old: jnp.where(passed, new, old), so_far, inside)
        before = combine(inside, before)
    return before


def pair_combine(preceding, later):
    return (preceding[0] * later[0], later[0][:, None, None] * preceding[1] + later[1])


def block_summary(inputs, masked, step_size, cumulative, b_matrix, c_matrix):
    row_count, columns = inputs.shape
    head_count = step_size.shape[0]
    x_heads = inputs.reshape(row_count, head_count, columns // head_count)
    dy_heads = masked.reshape(row_count, head_count, columns // head_count)
    to_end = jnp.exp(cumulative[:, -1:] - cumulative)
    into_state = (b_matrix.astype(jnp.float32)[None] * (to_end * step_size)[:, None, :]).astype(
        jnp.bfloat16
    )
    into_grad = (c_matrix.astype(jnp.float32)[None] * jnp.exp(cumulative)[:, None, :]).astype(
        jnp.bfloat16
    )
    state_part = jnp.einsum("hnu,uhp->hnp", into_state, x_heads, preferred_element_type=jnp.float32)
    grad_part = jnp.einsum("hnu,uhp->hnp", into_grad, dy_heads, preferred_element_type=jnp.float32)
    return (jnp.exp(cumulative[:, -1]), state_part, grad_part)


def block_grads(
    inputs,
    masked,
    step_size,
    cumulative,
    b_matrix,
    c_matrix,
    incoming_state,
    grad_in,
    skip_gain,
    scale_b,
    scale_c,
):
    row_count, columns = inputs.shape
    head_count = step_size.shape[0]
    head_dim = columns // head_count
    state_size = b_matrix.shape[0]
    group_size = math.gcd(head_count, 32)
    rounds = head_count // group_size
    to_end = jnp.exp(cumulative[:, -1:] - cumulative)
    from_start = jnp.exp(cumulative)
    causal = lax.broadcasted_iota(jnp.int32, (row_count, row_count), 0) >= lax.broadcasted_iota(
        jnp.int32, (row_count, row_count), 1
    )
    c_dot_b = jnp.dot(c_matrix.T, b_matrix, preferred_element_type=jnp.float32)
    grad16 = grad_in.astype(jnp.bfloat16)
    state16 = incoming_state.astype(jnp.bfloat16)

    def one_group(group_index, running):
        grad_x, mixing, cross_b, across_c_terms = running
        offset = group_index * group_size
        x_heads = lax.dynamic_slice_in_dim(
            inputs, offset * head_dim, group_size * head_dim, 1
        ).reshape(row_count, group_size, head_dim)
        dy_heads = lax.dynamic_slice_in_dim(
            masked, offset * head_dim, group_size * head_dim, 1
        ).reshape(row_count, group_size, head_dim)
        cums_group = lax.dynamic_slice_in_dim(cumulative, offset, group_size, 0)
        dt_group = lax.dynamic_slice_in_dim(step_size, offset, group_size, 0)
        end_group = lax.dynamic_slice_in_dim(to_end, offset, group_size, 0)
        start_group = lax.dynamic_slice_in_dim(from_start, offset, group_size, 0)
        gradient_group = lax.dynamic_slice_in_dim(grad16, offset, group_size, 0)
        state_group = lax.dynamic_slice_in_dim(state16, offset, group_size, 0)
        skip_group = lax.dynamic_slice_in_dim(skip_gain, offset, group_size, 0)
        differences = cums_group[:, :, None] - cums_group[:, None, :]
        forward_decay = jnp.exp(jnp.where(causal[None], differences, -jnp.inf))
        kernel = (forward_decay * c_dot_b[None]).astype(jnp.bfloat16)
        within = jnp.einsum("hut,uhp->thp", kernel, dy_heads, preferred_element_type=jnp.float32)
        across = (
            jnp.einsum("nt,hnp->thp", b_matrix, gradient_group, preferred_element_type=jnp.float32)
            * end_group.T[:, :, None]
        )
        pieces = dt_group.T[:, :, None] * (within + across) + skip_group[
            None, :, None
        ] * dy_heads.astype(jnp.float32)
        grad_x = lax.dynamic_update_slice_in_dim(
            grad_x,
            pieces.astype(jnp.bfloat16).reshape(row_count, group_size * head_dim),
            offset * head_dim,
            1,
        )
        scores = jnp.einsum("thp,uhp->htu", x_heads, dy_heads, preferred_element_type=jnp.float32)
        mixing = mixing + jnp.sum(
            dt_group[:, :, None] * jnp.swapaxes(forward_decay, 1, 2) * scores, axis=0
        )
        b_terms = jnp.einsum(
            "thp,hnp->htn", x_heads, gradient_group, preferred_element_type=jnp.float32
        )
        cross_b = cross_b + jnp.einsum(
            "htn,ht->nt", b_terms, dt_group * end_group, precision=HIGHEST
        )
        c_terms = jnp.einsum(
            "thp,hnp->htn", dy_heads, state_group, preferred_element_type=jnp.float32
        )
        across_c_terms = across_c_terms + jnp.einsum(
            "htn,ht->nt", c_terms, start_group, precision=HIGHEST
        )
        return (grad_x, mixing, cross_b, across_c_terms)

    initial = (
        jnp.zeros((row_count, columns), jnp.bfloat16),
        jnp.zeros((row_count, row_count), jnp.float32),
        jnp.zeros((state_size, row_count), jnp.float32),
        jnp.zeros((state_size, row_count), jnp.float32),
    )
    grad_x, mixing, cross_b, across_c_terms = lax.fori_loop(0, rounds, one_group, initial)
    grad_b = (
        jnp.dot(c_matrix.astype(jnp.float32), mixing.T, precision=HIGHEST) + cross_b
    ) * scale_b
    grad_c = (
        jnp.dot(b_matrix.astype(jnp.float32), mixing, precision=HIGHEST) + across_c_terms
    ) * scale_c
    return (grad_x, grad_b, grad_c)


def slab_grads(
    input_lines,
    dy_rows,
    dt_rows,
    cum_rows,
    b_rows,
    c_rows,
    state_blocks,
    grad_blocks,
    skip_part,
    scale_b,
    scale_c,
):
    tokens, columns = input_lines.shape
    head_count = dt_rows.shape[0]
    state_size = b_rows.shape[0]
    blocks = tokens // SPAN
    x_blocks = input_lines.reshape(blocks, SPAN, columns)
    dy_blocks = dy_rows.reshape(blocks, SPAN, columns)
    dt_blocks = dt_rows.reshape(head_count, blocks, SPAN).transpose(1, 0, 2)
    cum_blocks = cum_rows.reshape(head_count, blocks, SPAN).transpose(1, 0, 2)
    b_blocks = b_rows.reshape(state_size, blocks, SPAN).transpose(1, 0, 2)
    c_blocks = c_rows.reshape(state_size, blocks, SPAN).transpose(1, 0, 2)
    grad_x, grad_b, grad_c = lax.map(
        lambda element: block_grads(*element, skip_part, scale_b, scale_c),
        (x_blocks, dy_blocks, dt_blocks, cum_blocks, b_blocks, c_blocks, state_blocks, grad_blocks),
    )
    grad_x = grad_x.reshape(tokens, columns)
    grad_b = grad_b.transpose(1, 0, 2).reshape(state_size, tokens)
    grad_c = grad_c.transpose(1, 0, 2).reshape(state_size, tokens)
    return (grad_x, grad_b, grad_c)


def local(inputs, out_grad, step_size, log_decay, b_matrix, c_matrix, skip_gain, lengths):
    tokens = inputs.shape[1]
    columns = inputs.shape[2]
    head_count = step_size.shape[1]
    head_dim = columns // head_count
    state_size = b_matrix.shape[1]
    shard_count = lax.axis_size(SEQ)
    blocks = tokens // SPAN
    first_row = lax.axis_index(SEQ) * tokens
    interior = first_row + lax.iota(jnp.int32, tokens) < lengths[0]
    masked = jnp.where(interior[:, None], out_grad[0], jnp.zeros((), jnp.bfloat16))
    x_blocks = inputs[0].reshape(blocks, SPAN, columns)
    dy_blocks = masked.reshape(blocks, SPAN, columns)
    dt_blocks = step_size[0].reshape(head_count, blocks, SPAN).transpose(1, 0, 2)
    cum_rows = jnp.cumsum(log_decay[0].reshape(head_count, blocks, SPAN), axis=2).reshape(
        head_count, tokens
    )
    cumulative = cum_rows.reshape(head_count, blocks, SPAN).transpose(1, 0, 2)
    b_blocks = b_matrix[0].reshape(state_size, blocks, SPAN).transpose(1, 0, 2)
    c_blocks = c_matrix[0].reshape(state_size, blocks, SPAN).transpose(1, 0, 2)
    decays, state_parts, grad_parts = lax.map(
        lambda element: block_summary(*element),
        (x_blocks, dy_blocks, dt_blocks, cumulative, b_blocks, c_blocks),
    )

    def fold_blocks(running, element):
        totals, portion_sum = running
        factor, portion = element
        return ((totals * factor, factor[:, None, None] * portion_sum + portion), None)

    identity = (
        jnp.ones((head_count,), jnp.float32),
        jnp.zeros((head_count, state_size, head_dim), jnp.float32),
    )
    (whole_decay, state_total), _ = lax.scan(fold_blocks, identity, (decays, state_parts))
    (_, grad_total), _ = lax.scan(fold_blocks, identity, (decays, grad_parts), reverse=True)
    _, incoming_state = entering((whole_decay, state_total), SEQ, pair_combine, identity, False)
    _, grad_in = entering((whole_decay, grad_total), SEQ, pair_combine, identity, True)

    def pass_on(running, element):
        factor, portion = element
        return (factor[:, None, None] * running + portion, running)

    _, state_blocks = lax.scan(pass_on, incoming_state, (decays, state_parts))
    _, grad_blocks = lax.scan(pass_on, grad_in, (decays, grad_parts), reverse=True)
    scale_b = 1.0 / math.sqrt(columns)
    scale_c = math.sqrt(state_size / (columns * shard_count * tokens))
    grad_x, grad_b, grad_c = slab_grads(
        inputs[0],
        masked,
        step_size[0],
        cum_rows,
        b_matrix[0],
        c_matrix[0],
        state_blocks,
        grad_blocks,
        skip_gain,
        scale_b,
        scale_c,
    )
    return (grad_x[None], grad_b[None], grad_c[None])


def solution(mesh):
    torus = Mesh(mesh.devices.reshape(8, 4, mesh.shape["batch"]), ("seq_0", "seq_1", "batch"))
    placed = (
        P("batch", SEQ, None),
        P("batch", SEQ, None),
        P("batch", None, SEQ),
        P("batch", None, SEQ),
        P("batch", None, SEQ),
        P("batch", None, SEQ),
        P(),
        P("batch"),
    )
    return jax.shard_map(
        local,
        mesh=torus,
        in_specs=placed,
        out_specs=(P("batch", SEQ, None), P("batch", None, SEQ), P("batch", None, SEQ)),
        check_vma=False,
    )
```

profile of v0, /device:TPU:16, one launch (start us, length us, event | category | flops | bytes accessed | tf_op | source)
XLA Modules:
  0.0 325.8 jit_solution(2404002349363539723)
XLA Ops:
  11.8 3.2 copy.29
  15.1 2.7 fusion.30
  17.9 4.7 %copy.43 = bf16[1,256,6144]{1,2,0:T(8,128)(2,1)} copy(bf16[1,256,6144]{2,1,0:T(8,128)(2,1)} %param.10) | data formatting | bytes 6291456 | tf_op args[0]
  24.2 3.7 %convolution_add_fusion = f32[96,16,64]{2,1,0:T(8,128)} fusion(bf16[256,96,64]{0,2,1:T(8,128)(2,1)} %bitcast.47, f32[96,256]{1,0:T(8,128)S(1)} %get-tuple-element.681, f32[16,256]{1,0:T(8,128)S(1)} %bitcast_convert_fusion.1, f32[96]{0:T(128)S(1)} %exponential_multiply_fusion), kind=kOutput, calls=%fused_computation.49 | convolution fusion | flops 51216384 | bytes 3654016 | tf_op jit(solution)/shard_map/while/body/eval_jaxpr/hnu,uhp->hnp/dot_general | solution.py:53
  29.5 10.7 %all-reduce = f32[384]{0:T(512)S(1)} all-reduce(f32[384]{0:T(512)S(1)} %dynamic-update-slice), channel_id=2, replica_groups=mesh['seq_0'=8,'seq_1'=4,'batch'=8] {'seq_1'}, use_global_device_ids=true, to_apply=%add | all-reduce | flops 384 | bytes 3072
  40.4 22.5 %all-gather.14.cloned.1.call-done = f32[384,16,64]{2,1,0:T(8,128)} async-done(((f32[96,16,64]{2,1,0:T(8,128)}), f32[384,16,64]{2,1,0:T(8,128)}) %all-gather.14.cloned.1.call-update) | async-done | bytes 1572880 | tf_op jit(solution)/shard_map/all_gather | solution.py:27
  62.8 44.6 %all-gather.16.cloned.1.call-done = f32[384,16,64]{2,1,0:T(8,128)} async-done(((f32[96,16,64]{2,1,0:T(8,128)}), f32[384,16,64]{2,1,0:T(8,128)}) %all-gather.16.cloned.1.call-update) | async-done | bytes 1572880 | tf_op jit(solution)/shard_map/all_gather | solution.py:27
  107.4 4.1 %bitcast_add_fusion.10 = (f32[1,96,16,64]{3,2,1,0:T(8,128)}, f32[1,96,16,64]{3,2,1,0:T(8,128)}) fusion(f32[384,16,64]{2,1,0:T(8,128)} %all-gather.16.cloned.1.call-done, f32[96]{0:T(128)S(1)} %get-tuple-element.723, f32[96]{0:T(128)S(1)} %get-tuple-element.728, f32[96]{0:T(128)S(1)} %get-tuple-element.729, f32[96]{0:T(128)S(1)} %get-tuple-element.725, ...), kind=kLoop, calls=%fused_computation.71 | loop fusion | flops 1376256 | bytes 3934464 | tf_op jit(solution)/shard_map/add | solution.py:38
  116.2 16.9 %all-gather.4 = f32[8,1,96]{2,1,0:T(1,128)S(1)} all-gather(f32[1,1,96]{2,1,0:T(1,128)S(1)} %get-tuple-element.726), channel_id=1, replica_groups=mesh['seq_0'=8,'seq_1'=4,'batch'=8] {'seq_0'}, dimensions={0}, use_global_device_ids=true | all-gather | bytes 3456 | tf_op jit(solution)/shard_map/all_gather | solution.py:27
  133.1 14.7 %all-gather.3 = f32[8,1,96]{2,1,0:T(1,128)S(1)} all-gather(f32[1,1,96]{2,1,0:T(1,128)S(1)} %get-tuple-element.727), channel_id=1, replica_groups=mesh['seq_0'=8,'seq_1'=4,'batch'=8] {'seq_0'}, dimensions={0}, use_global_device_ids=true | all-gather | bytes 3456 | tf_op jit(solution)/shard_map/all_gather | solution.py:27
  150.6 18.3 %all-gather.12.cloned.1.call-done = f32[8,96,16,64]{1,3,2,0:T(8,128)} async-done(((f32[1,96,16,64]{1,3,2,0:T(8,128)}), f32[8,96,16,64]{1,3,2,0:T(8,128)}) %all-gather.12.cloned.1.call-update) | async-done | bytes 3145744 | tf_op jit(solution)/shard_map/all_gather | solution.py:27
  168.9 3.5 %fusion.70 = (f32[1,96,16,64]{1,3,2,0:T(8,128)}, f32[1,96,16,64]{1,3,2,0:T(8,128)S(1)}, f32[1,96,16,64]{1,3,2,0:T(8,128)S(1)}, f32[1,96,16,64]{1,3,2,0:T(8,128)S...) fusion(f32[8,96,16,64]{1,3,2,0:T(8,128)} %all-gather.12.cloned., ...), kind=kLoop, calls=%fused_computation.155 | loop fusion | bytes 6291456 | tf_op jit(solution)/shard_map/slice | solution.py:31
  174.7 2.3 copy.80
  184.4 40.1 %all-gather.10.cloned.1.call-done = f32[8,96,16,64]{1,3,2,0:T(8,128)} async-done(((f32[1,96,16,64]{1,3,2,0:T(8,128)}), f32[8,96,16,64]{1,3,2,0:T(8,128)}) %all-gather.10.cloned.1.call-update) | async-done | bytes 3145744 | tf_op jit(solution)/shard_map/all_gather | solution.py:27
  224.5 3.8 %fusion.71 = (f32[1,96,16,64]{1,3,2,0:T(8,128)S(1)}, f32[1,96,16,64]{1,3,2,0:T(8,128)}, f32[1,96,16,64]{1,3,2,0:T(8,128)}, f32[1,96,16,64]{1,3,2,0:T(8,128)}, f3...) fusion(f32[8,96,16,64]{1,3,2,0:T(8,128)} %all-gather.10.cloned., ...), kind=kLoop, calls=%fused_computation.156 | loop fusion | bytes 6291456 | tf_op jit(solution)/shard_map/slice | solution.py:31
  232.0 2.4 copy.74
  234.4 2.3 copy.75
  236.7 2.3 copy.76
  238.9 2.3 copy.77
  241.2 2.3 copy.78
  243.6 5.9 %fusion.42 = bf16[96,16,64]{2,1,0:T(8,128)(2,1)} fusion(f32[1,96,16,64]{3,2,1,0:T(8,128)} %copy.86, f32[1,96,16,64]{3,2,1,0:T(8,128)} %copy.85, f32[1,96,16,64]{3,2,1,0:T(8,128)} %copy.84, f32[1,96,16,64]{3,2,1,0:T(8,128)} %copy.83, f32[1,96,16,64]{3,2,1,0:T(8,128)} %copy.82, f32[1,96,16,64]{3,2,1,0:T(8,128)} %copy.81, f32[1,96,16,64]{3,2,1,0:T(8,128)} %copy.80, ...), kind=kLoop, calls=%fused_computation.63 | loop fusion | flops 3637248 | bytes 4920204 | tf_op jit(solution)/shard_map/while/body/eval_jaxpr/convert_element_type | solution.py:84
  249.5 2.7 fusion.49
  254.2 62.0 %while.21 = (s32[]{:T(128)}, bf16[256,6144]{1,0:T(8,128)(2,1)}, f32[256,256]{1,0:T(8,128)S(1)}, f32[16,256]{1,0:T(8,128)S(1)}, f32[16,256]{1,0:T(8,128)}, /*inde...) while((s32[]{:T(128)}, bf16[256,6144]{1,0:T(8,128)(2,1)}, ...), condition=%wide.region_4.5_spmd.clone.clone, body=%wide.region_2.4_spmd.clone.clone.sunk | while | flops 610484224 | bytes 30188352 | solution.py:143
  255.0 2.8 fusion.104
  261.1 4.4 %fusion.105 = bf16[256,32,64]{0,2,1:T(8,128)(2,1)} fusion(f32[32,64,256]{2,1,0:T(8,128)S(1)} %copy-done, bf16[256,32,64]{0,2,1:T(8,128)(2,1)S(1)} %bitcast.325, f32[256,256]{1,0:T(8,128)} %get-tuple-element.894, f32[32,256]{1,0:T(8,128)S(1)} %constant_dynamic-slice_fusion.8, pred[256,256]{1,0:T(8,128)(4,1)S(1)} %iota_compare_fusion.2, ...), kind=kOutput, calls=%fused_computation.13.clone.1 | convolution fusion | flops 280494080 | bytes 4620416 | tf_op jit(solution)/shard_map/while/body/eval_jaxpr/while/body/eval_jaxpr/hut,uhp->thp/dot_general | solution.py:105
  268.2 3.5 %multiply_reduce_fusion.2 = f32[256,256]{1,0:T(8,128)S(1)} fusion(f32[32,256]{1,0:T(8,128)S(1)} %get-tuple-element.838, f32[32,256]{1,0:T(8,128)S(1)} %constant_dynamic-slice_fusion.8, pred[256,256]{1,0:T(8,128)(4,1)S(1)} %copy.96, bf16[256,32,64]{0,2,1:T(8,128)(2,1)S(1)} %bitcast.328, bf16[256,32,64]{0,2,1:T(8,128)(2,1)S(1)} %bitcast.326), kind=kOutput, calls=%fused_computation.1.clone.1 | convolution fusion | flops 278855680 | bytes 2490368 | tf_op jit(solution)/shard_map/while/body/eval_jaxpr/while/body/eval_jaxpr/thp,uhp->htu/dot_general | solution.py:119
  275.6 2.8 fusion.104
  281.8 4.4 %fusion.105 = bf16[256,32,64]{0,2,1:T(8,128)(2,1)} fusion(f32[32,64,256]{2,1,0:T(8,128)S(1)} %copy-done, bf16[256,32,64]{0,2,1:T(8,128)(2,1)S(1)} %bitcast.325, f32[256,256]{1,0:T(8,128)} %get-tuple-element.894, f32[32,256]{1,0:T(8,128)S(1)} %constant_dynamic-slice_fusion.8, pred[256,256]{1,0:T(8,128)(4,1)S(1)} %iota_compare_fusion.2, ...), kind=kOutput, calls=%fused_computation.13.clone.1 | convolution fusion | flops 280494080 | bytes 4620416 | tf_op jit(solution)/shard_map/while/body/eval_jaxpr/while/body/eval_jaxpr/hut,uhp->thp/dot_general | solution.py:105
  288.9 3.5 %multiply_reduce_fusion.2 = f32[256,256]{1,0:T(8,128)S(1)} fusion(f32[32,256]{1,0:T(8,128)S(1)} %get-tuple-element.838, f32[32,256]{1,0:T(8,128)S(1)} %constant_dynamic-slice_fusion.8, pred[256,256]{1,0:T(8,128)(4,1)S(1)} %copy.96, bf16[256,32,64]{0,2,1:T(8,128)(2,1)S(1)} %bitcast.328, bf16[256,32,64]{0,2,1:T(8,128)(2,1)S(1)} %bitcast.326), kind=kOutput, calls=%fused_computation.1.clone.1 | convolution fusion | flops 278855680 | bytes 2490368 | tf_op jit(solution)/shard_map/while/body/eval_jaxpr/while/body/eval_jaxpr/thp,uhp->htu/dot_general | solution.py:119
  296.3 2.8 fusion.104
  302.4 4.4 %fusion.105 = bf16[256,32,64]{0,2,1:T(8,128)(2,1)} fusion(f32[32,64,256]{2,1,0:T(8,128)S(1)} %copy-done, bf16[256,32,64]{0,2,1:T(8,128)(2,1)S(1)} %bitcast.325, f32[256,256]{1,0:T(8,128)} %get-tuple-element.894, f32[32,256]{1,0:T(8,128)S(1)} %constant_dynamic-slice_fusion.8, pred[256,256]{1,0:T(8,128)(4,1)S(1)} %iota_compare_fusion.2, ...), kind=kOutput, calls=%fused_computation.13.clone.1 | convolution fusion | flops 280494080 | bytes 4620416 | tf_op jit(solution)/shard_map/while/body/eval_jaxpr/while/body/eval_jaxpr/hut,uhp->thp/dot_general | solution.py:105
  309.6 3.5 %multiply_reduce_fusion.2 = f32[256,256]{1,0:T(8,128)S(1)} fusion(f32[32,256]{1,0:T(8,128)S(1)} %get-tuple-element.838, f32[32,256]{1,0:T(8,128)S(1)} %constant_dynamic-slice_fusion.8, pred[256,256]{1,0:T(8,128)(4,1)S(1)} %copy.96, bf16[256,32,64]{0,2,1:T(8,128)(2,1)S(1)} %bitcast.328, bf16[256,32,64]{0,2,1:T(8,128)(2,1)S(1)} %bitcast.326), kind=kOutput, calls=%fused_computation.1.clone.1 | convolution fusion | flops 278855680 | bytes 2490368 | tf_op jit(solution)/shard_map/while/body/eval_jaxpr/while/body/eval_jaxpr/thp,uhp->htu/dot_general | solution.py:119
  (148 shorter events, 62.4 us)
Async XLA Ops:
  7.2 55.7 %all-gather.14.cloned.1.call-start = ((), (), s32[]{:S(2)}) async-start(), calls=%async_computation.2 | async-start | bytes 3932160 | tf_op jit(solution)/shard_map/all_gather | solution.py:27
  11.8 3.2 copy-start.15
  15.0 2.8 copy-start.16
  17.8 4.7 %copy-start.13 = (bf16[1,16,256]{2,1,0:T(8,128)(2,1)S(1)}, bf16[1,16,256]{2,1,0:T(8,128)(2,1)}, u32[]{:S(2)}) copy-start(bf16[1,16,256]{2,1,0:T(8,128)(2,1)} %param.14) | copy-start | bytes 24580
  17.8 89.6 %all-gather.16.cloned.1.call-start = ((), (), s32[]{:S(2)}) async-start(), calls=%async_computation.3 | async-start | bytes 3932160 | tf_op jit(solution)/shard_map/all_gather | solution.py:27
  22.5 5.5 %copy-start.18 = (u32[256]{0:T(256)S(1)}, u32[256]{0:T(256)}, u32[]{:S(2)}) copy-start(u32[256]{0:T(256)} %constant.204) | copy-start | bytes 3076
  28.0 141.0 %all-gather.12.cloned.1.call-start = ((), (), s32[]{:S(2)}) async-start(), calls=%async_computation.1 | async-start | bytes 4718592 | tf_op jit(solution)/shard_map/all_gather | solution.py:27
  111.5 37.2 %copy-start.17 = (pred[256]{0:T(512)(128)(4,1)S(1)}, pred[256]{0:T(512)(128)(4,1)}, u32[]{:S(2)}) copy-start(pred[256]{0:T(512)(128)(4,1)} %copy-done.16) | copy-start | bytes 772
  113.8 110.8 %all-gather.10.cloned.1.call-start = ((), (), s32[]{:S(2)}) async-start(), calls=%async_computation | async-start | bytes 4718592 | tf_op jit(solution)/shard_map/all_gather | solution.py:27
  232.0 11.5 %copy-start.2 = (f32[384,16,64]{2,1,0:T(8,128)S(1)}, f32[384,16,64]{2,1,0:T(8,128)}, u32[]{:S(2)}) copy-start(f32[384,16,64]{2,1,0:T(8,128)} %all-gather.16.cloned.1.call-done) | copy-start | bytes 4718596
  243.5 5.9 %copy-start.1 = (f32[384,16,64]{2,1,0:T(8,128)S(1)}, f32[384,16,64]{2,1,0:T(8,128)}, u32[]{:S(2)}) copy-start(f32[384,16,64]{2,1,0:T(8,128)} %all-gather.14.cloned.1.call-done) | copy-start | bytes 4718596
  243.5 5.9 %copy-start.3 = (f32[1,96,16,64]{3,2,1,0:T(8,128)S(1)}, f32[1,96,16,64]{3,2,1,0:T(8,128)}, u32[]{:S(2)}) copy-start(f32[1,96,16,64]{3,2,1,0:T(8,128)} %copy.71) | copy-start | bytes 1179652
  243.5 5.9 %copy-start.4 = (f32[1,96,16,64]{3,2,1,0:T(8,128)S(1)}, f32[1,96,16,64]{3,2,1,0:T(8,128)}, u32[]{:S(2)}) copy-start(f32[1,96,16,64]{3,2,1,0:T(8,128)} %copy.72) | copy-start | bytes 1179652
  243.5 5.9 %copy-start.5 = (f32[1,96,16,64]{3,2,1,0:T(8,128)S(1)}, f32[1,96,16,64]{3,2,1,0:T(8,128)}, u32[]{:S(2)}) copy-start(f32[1,96,16,64]{3,2,1,0:T(8,128)} %copy.73) | copy-start | bytes 1179652
  243.5 5.9 %copy-start.6 = (f32[1,96,16,64]{3,2,1,0:T(8,128)S(1)}, f32[1,96,16,64]{3,2,1,0:T(8,128)}, u32[]{:S(2)}) copy-start(f32[1,96,16,64]{3,2,1,0:T(8,128)} %copy.74) | copy-start | bytes 1179652
  243.5 5.9 %copy-start.7 = (f32[1,96,16,64]{3,2,1,0:T(8,128)S(1)}, f32[1,96,16,64]{3,2,1,0:T(8,128)}, u32[]{:S(2)}) copy-start(f32[1,96,16,64]{3,2,1,0:T(8,128)} %copy.75) | copy-start | bytes 1179652
  243.5 5.9 %copy-start.8 = (f32[1,96,16,64]{3,2,1,0:T(8,128)S(1)}, f32[1,96,16,64]{3,2,1,0:T(8,128)}, u32[]{:S(2)}) copy-start(f32[1,96,16,64]{3,2,1,0:T(8,128)} %copy.76) | copy-start | bytes 1179652
  243.5 5.9 %copy-start.9 = (f32[1,96,16,64]{3,2,1,0:T(8,128)S(1)}, f32[1,96,16,64]{3,2,1,0:T(8,128)}, u32[]{:S(2)}) copy-start(f32[1,96,16,64]{3,2,1,0:T(8,128)} %copy.77) | copy-start | bytes 1179652
  243.5 5.9 %copy-start.10 = (f32[1,96,16,64]{3,2,1,0:T(8,128)S(1)}, f32[1,96,16,64]{3,2,1,0:T(8,128)}, u32[]{:S(2)}) copy-start(f32[1,96,16,64]{3,2,1,0:T(8,128)} %copy.78) | copy-start | bytes 1179652
  258.5 2.6 copy-start
  271.7 2.5 copy-start.11
  271.7 3.1 copy-start.14
  274.2 0.6 copy-start.12
  279.2 2.6 copy-start
  292.4 2.5 copy-start.11
  292.4 3.1 copy-start.14
  294.9 0.6 copy-start.12
  299.8 2.6 copy-start
  313.0 2.5 copy-start.11
  313.1 3.1 copy-start.14
  315.5 0.6 copy-start.12
Sparse Core Ops, SparseCore 0:
  17.9 44.8 all-gather.13
  65.2 42.1 all-gather.15
  113.9 55.0 all-gather.11
  171.2 53.3 all-gather.9
where the time goes:
time: 328 us; the launch traced here: 326 us
  waiting for transfers between devices  126 us (38%)
  local copies, waits for them, and re-layouts  72.1 us (22%)
  matrix products  49.4 us (15%)
  blocking collectives  42.2 us (13%)
  other arithmetic  20.5 us (6%)
  between operations  15.5 us (5%)
    all_gather x4, waiting for transfers between devices, entering(): pieces = jax.tree.map(lambda part: lax.all_gather(part, axis), so_far)  125 us
    unnamed x51, local copies, waits for them, and re-layouts  35.9 us
    all_gather x2, blocking collectives, entering(): pieces = jax.tree.map(lambda part: lax.all_gather(part, axis), so_far)  31.6 us
    dot_general x3, matrix products, one_group(): jnp.einsum('hut,uhp->thp', kernel, dy_heads, preferred_element_type=jnp.f...  13.1 us
    unnamed x1, blocking collectives  10.7 us
    dot_general x3, matrix products, one_group(): jnp.einsum('thp,uhp->htu', x_heads, dy_heads, preferred_element_type=jnp....  10.5 us
    dot_general x3, matrix products, one_group(): jnp.einsum('nt,hnp->thp', b_matrix, gradient_group, preferred_element_typ...  8.36 us
    dynamic_update_slice x6, local copies, waits for them, and re-layouts, one_group(): lax.dynamic_update_slice_in_dim(grad_x, pieces.astype(jnp.bfloat16).resha...  7.58 us
  transfers between devices with their start and end apart: 4, of which 4 were waited for; matrix products, arithmetic and copies ran while one was open for 10% of the time, Pallas kernels for 0%

commit v1 on v0

v1 whole, which is shorter than its diff:
```python
import math

import jax
import jax.numpy as jnp
from jax import lax
from jax.experimental import pallas as pl
from jax.experimental.pallas import tpu as pltpu
from jax.sharding import PartitionSpec as P

MESH = pl.DeviceIdType.MESH
HIGHEST = lax.Precision.HIGHEST
LOG2E = 1.4426950408889634
SPAN = 256
HALF = 128
STATE = 16
HEADS_PER_GROUP = 6
LANES = 384
GROUPS = 16
PEERS = 32
LOAD_CHUNKS = 4
FIRST_WINDOW = 9
NT = (((1,), (1,)), ((), ()))


def nt_dot(a, b, precision=None):
    return lax.dot_general(a, b, NT, precision=precision, preferred_element_type=jnp.float32)


def plain_dot(a, b, precision=None):
    return jnp.dot(a, b, precision=precision, preferred_element_type=jnp.float32)


def kernel(
    scale_b,
    scale_c,
    length_ref,
    skip_ref,
    x_hbm,
    dy_hbm,
    dt_ref,
    decay_ref,
    b_ref,
    c_ref,
    gx_ref,
    gb_ref,
    gc_ref,
    xv,
    dyv,
    partial_x,
    row_s,
    col_s,
    to_end_s,
    from_start_s,
    cb_s,
    mix_s,
    parts_out,
    parts_in,
    ends_out,
    ends_in,
    scan_g,
    ends_wide,
    states_out,
    states_in,
    load_x_sem,
    load_dy_sem,
    sems,
):
    me = lax.axis_index("seq")
    lane_of_batch = lax.axis_index("batch")

    def peer(k):
        return lax.rem(me + k, PEERS)

    chunk = 6144 // LOAD_CHUNKS
    loads_x, loads_dy = [], []
    for i in range(LOAD_CHUNKS):
        part = pl.ds(i * chunk, chunk)
        loads_x.append(pltpu.make_async_copy(x_hbm.at[0, :, part], xv.at[:, part], load_x_sem.at[i]))
        loads_dy.append(
            pltpu.make_async_copy(dy_hbm.at[0, :, part], dyv.at[:, part], load_dy_sem.at[i])
        )
    for i in range(LOAD_CHUNKS):
        loads_x[i].start()
        loads_dy[i].start()

    barrier = pltpu.get_barrier_semaphore()

    def greet(k, carry):
        pl.semaphore_signal(
            barrier, inc=1, device_id=(peer(k), lane_of_batch), device_id_type=MESH
        )
        return carry

    lax.fori_loop(1, PEERS, greet, 0)

    decay = decay_ref[0]
    dt = dt_ref[0]
    rows = lax.broadcasted_iota(jnp.int32, (SPAN, SPAN), 0)
    cols = lax.broadcasted_iota(jnp.int32, (SPAN, SPAN), 1)
    cum = plain_dot(decay, (rows <= cols).astype(jnp.float32), HIGHEST)
    from_start = jnp.exp(cum)
    to_end = dt * jnp.exp(cum[:, SPAN - 1 :] - cum)
    row_log = cum * LOG2E
    col_log = row_log - jnp.log(dt) * LOG2E
    for g in range(GROUPS):
        take = slice(g * HEADS_PER_GROUP, (g + 1) * HEADS_PER_GROUP)
        row_s[g, 0:HEADS_PER_GROUP, :] = row_log[take]
        col_s[g, 0:HEADS_PER_GROUP, :] = col_log[take]
        to_end_s[g, 0:HEADS_PER_GROUP, :] = to_end[take]
        from_start_s[g, 0:HEADS_PER_GROUP, :] = from_start[take]
    padded = jnp.concatenate([decay, jnp.zeros((32, SPAN), jnp.float32)], axis=0)
    total = nt_dot(jnp.ones((8, SPAN), jnp.float32), padded, HIGHEST)
    ends_out[...] = jnp.exp(total[0:1])
    b_wide = b_ref[0].astype(jnp.float32)
    c_wide = c_ref[0].astype(jnp.float32)
    b_turned = jnp.transpose(b_wide).astype(jnp.bfloat16)
    cb_s[...] = plain_dot(b_turned, c_ref[0])
    mix_s[...] = jnp.zeros_like(mix_s)

    position = lax.broadcasted_iota(jnp.int32, (SPAN, 1), 0) + me * SPAN
    valid = (position < length_ref[0]).astype(jnp.float32).astype(jnp.bfloat16)
    low = lax.broadcasted_iota(jnp.int32, (STATE, HALF), 1) < 64

    def lanes_of(g):
        return pl.ds(pl.multiple_of(g * LANES, HALF), LANES)

    def per_head(wide, weights):
        return jnp.concatenate(
            [(wide * weights[k : k + 1, :]).astype(jnp.bfloat16) for k in range(HEADS_PER_GROUP)],
            axis=0,
        )

    def own_heads(product):
        pieces = []
        for k in range(3):
            block = product[32 * k : 32 * k + 32, HALF * k : HALF * k + HALF]
            pieces.append(jnp.where(low, block[:STATE], block[STATE:]))
        return jnp.concatenate(pieces, axis=1)

    def summary(g, carry):
        lanes = lanes_of(g)
        dy = dyv[:, lanes] * valid
        dyv[:, lanes] = dy
        state = own_heads(plain_dot(per_head(b_wide, to_end_s[g]), xv[:, lanes]))
        grad = own_heads(plain_dot(per_head(c_wide, from_start_s[g]), dy))
        for half in range(2):
            take = slice(8 * half, 8 * half + 8)
            parts_out[2 * g + half] = jnp.concatenate([state[take], grad[take]], axis=0).astype(
                jnp.bfloat16
            )
        return carry

    per_chunk = GROUPS // LOAD_CHUNKS
    for i in range(LOAD_CHUNKS):
        loads_x[i].wait()
        loads_dy[i].wait()
        lax.fori_loop(i * per_chunk, (i + 1) * per_chunk, summary, 0)

    pl.semaphore_wait(barrier, PEERS - 1)

    def copy_parts(j):
        return pltpu.make_async_remote_copy(
            src_ref=parts_out.at[j],
            dst_ref=parts_in.at[me],
            send_sem=sems.at[0],
            recv_sem=sems.at[1],
            device_id=(j, lane_of_batch),
            device_id_type=MESH,
        )

    def copy_ends(j):
        return pltpu.make_async_remote_copy(
            src_ref=ends_out,
            dst_ref=ends_in.at[me],
            send_sem=sems.at[2],
            recv_sem=sems.at[3],
            device_id=(j, lane_of_batch),
            device_id_type=MESH,
        )

    def copy_states(j):
        return pltpu.make_async_remote_copy(
            src_ref=states_out.at[j],
            dst_ref=states_in.at[me],
            send_sem=sems.at[4],
            recv_sem=sems.at[5],
            device_id=(j, lane_of_batch),
            device_id_type=MESH,
        )

    def all_of(out_ref, in_ref, send, recv):
        return pltpu.make_async_remote_copy(
            src_ref=out_ref.at[pl.ds(0, PEERS - 1)],
            dst_ref=in_ref.at[pl.ds(0, PEERS - 1)],
            send_sem=sems.at[send],
            recv_sem=sems.at[recv],
            device_id=(peer(1), lane_of_batch),
            device_id_type=MESH,
        )

    def send_first(k, carry):
        copy_ends(peer(k)).start()
        copy_parts(peer(k)).start()
        return carry

    lax.fori_loop(1, PEERS, send_first, 0)
    parts_in[me] = parts_out[me]
    ends_in[me] = ends_out[...]

    causal = lax.broadcasted_iota(jnp.int32, (HALF, HALF), 0) <= lax.broadcasted_iota(
        jnp.int32, (HALF, HALF), 1
    )
    lane_row = lax.broadcasted_iota(jnp.int32, (1, HALF), 1)
    keep = (
        (lane_row < 64).astype(jnp.float32).astype(jnp.bfloat16),
        (lane_row >= 64).astype(jnp.float32).astype(jnp.bfloat16),
    )

    def within(g, carry):
        turned = jnp.transpose(col_s[g])
        logs = row_s[g]
        mix_aa = jnp.zeros((HALF, HALF), jnp.float32)
        mix_ab = jnp.zeros((HALF, HALF), jnp.float32)
        mix_bb = jnp.zeros((HALF, HALF), jnp.float32)
        for pair in range(3):
            lanes = pl.ds(pl.multiple_of(g * LANES + pair * HALF, HALF), HALF)
            x = xv[:, lanes]
            dy = dyv[:, lanes]
            first = jnp.zeros((HALF, HALF), jnp.float32)
            second = jnp.zeros((HALF, HALF), jnp.float32)
            for side in range(2):
                k = 2 * pair + side
                dy_one = dy * keep[side]
                score_a = nt_dot(x[:HALF], dy_one)
                score_b = nt_dot(x[HALF:], dy_one[HALF:])
                gap_aa = logs[k : k + 1, :HALF] - turned[:HALF, k : k + 1]
                gap_ab = logs[k : k + 1, HALF:] - turned[:HALF, k : k + 1]
                gap_bb = logs[k : k + 1, HALF:] - turned[HALF:, k : k + 1]
                fade_aa = jnp.exp2(jnp.where(causal, gap_aa, -jnp.inf))
                fade_ab = jnp.exp2(gap_ab)
                fade_bb = jnp.exp2(jnp.where(causal, gap_bb, -jnp.inf))
                mix_aa += fade_aa * score_a[:, :HALF]
                mix_ab += fade_ab * score_a[:, HALF:]
                mix_bb += fade_bb * score_b
                kernel_a = jnp.concatenate(
                    [
                        (fade_aa * cb_s[:HALF, :HALF]).astype(jnp.bfloat16),
                        (fade_ab * cb_s[:HALF, HALF:]).astype(jnp.bfloat16),
                    ],
                    axis=1,
                )
                kernel_b = (fade_bb * cb_s[HALF:, HALF:]).astype(jnp.bfloat16)
                first += plain_dot(kernel_a, dy_one)
                second += plain_dot(kernel_b, dy_one[HALF:])
            skip = jnp.where(
                lane_row < 64,
                skip_ref[HEADS_PER_GROUP * g + 2 * pair],
                skip_ref[HEADS_PER_GROUP * g + 2 * pair + 1],
            )
            direct = skip * dy.astype(jnp.float32)
            partial_x[:HALF, lanes] = first + direct[:HALF]
            partial_x[HALF:, lanes] = second + direct[HALF:]
        mix_s[:HALF, :HALF] += mix_aa
        mix_s[:HALF, HALF:] += mix_ab
        mix_s[HALF:, HALF:] += mix_bb
        return carry

    lax.fori_loop(0, FIRST_WINDOW, within, 0)

    all_of(parts_out, parts_in, 0, 1).wait_recv()
    all_of(ends_in, ends_in, 2, 3).wait_recv()

    head_row = lax.broadcasted_iota(jnp.int32, (HALF, LANES), 0)
    lane_head = lax.broadcasted_iota(jnp.int32, (HALF, LANES), 1) // 64
    mine = (head_row == lane_head + (me // 2) * HEADS_PER_GROUP).astype(jnp.float32)
    gathered = jnp.concatenate([ends_in[i] for i in range(PEERS)], axis=0)
    ends_wide[...] = plain_dot(gathered, mine, HIGHEST)

    running = jnp.zeros((8, LANES), jnp.float32)
    for i in reversed(range(PEERS)):
        scan_g[i] = running
        running = ends_wide[i : i + 1, :] * running + parts_in[i].astype(jnp.float32)[8:]
    running = jnp.zeros((8, LANES), jnp.float32)
    for i in range(PEERS):
        states_out[i] = jnp.concatenate([running, scan_g[i]], axis=0).astype(jnp.bfloat16)
        running = ends_wide[i : i + 1, :] * running + parts_in[i].astype(jnp.float32)[:8]

    def send_second(k, carry):
        copy_states(peer(k)).start()
        return carry

    lax.fori_loop(1, PEERS, send_second, 0)
    states_in[me] = states_out[me]

    lax.fori_loop(FIRST_WINDOW, GROUPS, within, 0)

    all_of(states_out, states_in, 4, 5).wait_recv()

    def spread(rows16):
        blocks = []
        for k in range(3):
            tile = rows16[:, HALF * k : HALF * k + HALF]
            pad = [jnp.zeros((32, HALF), jnp.bfloat16)] * 3
            pad[k] = jnp.concatenate([tile * keep[0], tile * keep[1]], axis=0)
            blocks.append(jnp.concatenate(pad, axis=1))
        return jnp.concatenate(blocks, axis=0)

    def across(g, carry):
        cross_b, cross_c = carry
        lanes = lanes_of(g)
        even = states_in[2 * g].astype(jnp.float32)
        odd = states_in[2 * g + 1].astype(jnp.float32)
        state = spread(jnp.concatenate([even[:8], odd[:8]], axis=0).astype(jnp.bfloat16))
        grad = spread(jnp.concatenate([even[8:], odd[8:]], axis=0).astype(jnp.bfloat16))
        ends = to_end_s[g]
        starts = from_start_s[g]
        into = jnp.concatenate(
            [b_wide * ends[k : k + 1, :] for k in range(HEADS_PER_GROUP)], axis=0
        )
        term = plain_dot(jnp.transpose(into).astype(jnp.bfloat16), grad)
        gx_ref[0, :, lanes] = (partial_x[:, lanes] + term).astype(jnp.bfloat16)
        from_x = nt_dot(grad, xv[:, lanes])
        from_dy = nt_dot(state, dyv[:, lanes])
        for k in range(HEADS_PER_GROUP):
            take = slice(STATE * k, STATE * k + STATE)
            cross_b += from_x[take] * ends[k : k + 1, :]
            cross_c += from_dy[take] * starts[k : k + 1, :]
        return cross_b, cross_c

    zero = jnp.zeros((STATE, SPAN), jnp.float32)
    cross_b, cross_c = lax.fori_loop(0, GROUPS, across, (zero, zero))
    mixing = mix_s[...]
    gb_ref[0] = (nt_dot(c_wide, mixing, HIGHEST) + cross_b) * scale_b
    gc_ref[0] = (plain_dot(b_wide, mixing, HIGHEST) + cross_c) * scale_c

    all_of(parts_out, parts_in, 0, 1).wait_send()
    all_of(ends_in, ends_in, 2, 3).wait_send()
    all_of(states_out, states_in, 4, 5).wait_send()


def solution(mesh):
    def local(inputs, out_grad, step_size, log_decay, b_matrix, c_matrix, skip_gain, lengths):
        columns = inputs.shape[2]
        scale_b = 1.0 / math.sqrt(columns)
        scale_c = math.sqrt(STATE / (columns * PEERS * SPAN))
        vmem = pl.BlockSpec(memory_space=pltpu.VMEM)
        smem = pl.BlockSpec(memory_space=pltpu.SMEM)
        whole = pl.BlockSpec(memory_space=pl.ANY)
        f32, bf16 = jnp.float32, jnp.bfloat16
        return pl.pallas_call(
            lambda *refs: kernel(scale_b, scale_c, *refs),
            out_shape=(
                jax.ShapeDtypeStruct(inputs.shape, bf16),
                jax.ShapeDtypeStruct(b_matrix.shape, f32),
                jax.ShapeDtypeStruct(c_matrix.shape, f32),
            ),
            in_specs=[smem, smem, whole, whole, vmem, vmem, vmem, vmem],
            out_specs=(vmem, vmem, vmem),
            scratch_shapes=[
                pltpu.VMEM((SPAN, columns), bf16),
                pltpu.VMEM((SPAN, columns), bf16),
                pltpu.VMEM((SPAN, columns), f32),
                pltpu.VMEM((GROUPS, 8, SPAN), f32),
                pltpu.VMEM((GROUPS, 8, SPAN), f32),
                pltpu.VMEM((GROUPS, 8, SPAN), f32),
                pltpu.VMEM((GROUPS, 8, SPAN), f32),
                pltpu.VMEM((SPAN, SPAN), f32),
                pltpu.VMEM((SPAN, SPAN), f32),
                pltpu.VMEM((PEERS, 16, LANES), bf16),
                pltpu.VMEM((PEERS, 16, LANES), bf16),
                pltpu.VMEM((1, HALF), f32),
                pltpu.VMEM((PEERS, 1, HALF), f32),
                pltpu.VMEM((PEERS, 8, LANES), f32),
                pltpu.VMEM((PEERS, LANES), f32),
                pltpu.VMEM((PEERS, 16, LANES), bf16),
                pltpu.VMEM((PEERS, 16, LANES), bf16),
                pltpu.SemaphoreType.DMA((LOAD_CHUNKS,)),
                pltpu.SemaphoreType.DMA((LOAD_CHUNKS,)),
                pltpu.SemaphoreType.DMA((6,)),
            ],
            compiler_params=pltpu.CompilerParams(
                collective_id=0, has_side_effects=True, vmem_limit_bytes=48 * 1024 * 1024
            ),
        )(lengths, skip_gain, inputs, out_grad, step_size, log_decay, b_matrix, c_matrix)

    return jax.shard_map(
        local,
        mesh=mesh,
        in_specs=(
            P("batch", "seq", None),
            P("batch", "seq", None),
            P("batch", None, "seq"),
            P("batch", None, "seq"),
            P("batch", None, "seq"),
            P("batch", None, "seq"),
            P(),
            P("batch"),
        ),
        out_specs=(P("batch", "seq", None), P("batch", None, "seq"), P("batch", None, "seq")),
        check_vma=False,
    )
```

time: 328 us -> 48.3 us (0.15)
  waiting for transfers between devices: 126 us -> 0 us
  local copies, waits for them, and re-layouts: 72.1 us -> 6.7 us
  matrix products: 49.4 us -> 0 us
  blocking collectives: 42.2 us -> 0 us
  Pallas kernels: 0 us -> 40.1 us
  other arithmetic: 20.5 us -> 0 us
  between operations: 15.5 us -> 1.3 us
    all_gather x4 -> x0, waiting for transfers between devices: 125 us -> none  [entering(): pieces = jax.tree.map(lambda part: lax.all_gather(part, axis), so_far)]
    dot_general x20 -> x0, matrix products: 49.4 us -> none  [the longest x3 13.1 us: one_group(): jnp.einsum('hut,uhp->thp', kernel, dy_heads, preferred_element_type=jnp.f...]
    pallas_call x0 -> x1, Pallas kernels: none -> 40.1 us  [local(): pl.pallas_call(lambda *refs: kernel(scale_b, scale_c, *refs), out_shape=(...]
    all_gather x2 -> x0, blocking collectives: 31.6 us -> none  [entering(): pieces = jax.tree.map(lambda part: lax.all_gather(part, axis), so_far)]
    unnamed x51 -> x13, local copies, waits for them, and re-layouts: 35.9 us -> 6.7 us
    unnamed x1 -> x0, blocking collectives: 10.7 us -> none
    dynamic_slice x9 -> x0, local copies, waits for them, and re-layouts: 9.96 us -> none  [the longest x3 5.48 us: one_group(): lax.dynamic_slice_in_dim(inputs, offset * head_dim, group_size * head_dim...]
    convert_element_type x2 -> x0, other arithmetic: 8.52 us -> none  [the longest x1 5.86 us: block_grads(): state16 = incoming_state.astype(jnp.bfloat16)]
  transfers between devices with their start and end apart: 4 -> 0, of which waited for: 4 -> 0; matrix products, arithmetic and copies ran while one was open for 10% -> 0% of each run, Pallas kernels for 0% -> 0%
where the time goes in v1:
time: 48.3 us; the launch traced here: 48.1 us
  Pallas kernels  40.1 us (83%)
  local copies, waits for them, and re-layouts  6.7 us (14%)
  between operations  1.3 us (3%)
    pallas_call x1, Pallas kernels, local(): pl.pallas_call(lambda *refs: kernel(scale_b, scale_c, *refs), out_shape=(...  40.1 us
    unnamed x13, local copies, waits for them, and re-layouts  6.7 us

profile of v1, /device:TPU:16, one launch (start us, length us, event | category | flops | bytes accessed | tf_op | source)
XLA Modules:
  0.0 48.1 jit_solution(3298628769060606844)
XLA Ops:
  1.3 0.0 copy-start
  1.3 0.9 %copy-done = f32[1,96,256]{2,1,0:T(8,128)S(1)} copy-done((f32[1,96,256]{2,1,0:T(8,128)S(1)}, f32[1,96,256]{2,1,0:T(8,128)}, u32[]{:S(2)}) %copy-start) | copy-done | bytes 98328
  2.2 0.0 copy-start.1
  2.2 0.9 %copy-done.1 = f32[1,96,256]{2,1,0:T(8,128)S(1)} copy-done((f32[1,96,256]{2,1,0:T(8,128)S(1)}, f32[1,96,256]{2,1,0:T(8,128)}, u32[]{:S(2)}) %copy-start.1) | copy-done | bytes 98328
  3.1 0.0 copy-start.2
  3.1 0.7 %copy-done.2 = bf16[1,16,256]{2,1,0:T(8,128)(2,1)S(1)} copy-done((bf16[1,16,256]{2,1,0:T(8,128)(2,1)S(1)}, bf16[1,16,256]{2,1,0:T(8,128)(2,1)}, u32[]{:S(2)}) %copy-start.2) | copy-done | bytes 8216
  3.8 0.0 copy-start.3
  3.8 0.7 %copy-done.3 = bf16[1,16,256]{2,1,0:T(8,128)(2,1)S(1)} copy-done((bf16[1,16,256]{2,1,0:T(8,128)(2,1)S(1)}, bf16[1,16,256]{2,1,0:T(8,128)(2,1)}, u32[]{:S(2)}) %copy-start.3) | copy-done | bytes 8216
  4.5 0.0 copy-start.4
  4.5 0.7 %copy-done.4 = f32[96]{0:T(128)S(1)} copy-done((f32[96]{0:T(128)S(1)}, f32[96]{0:T(128)}, u32[]{:S(2)}) %copy-start.4) | copy-done | bytes 408
  5.1 40.1 %shard_map.103 = (bf16[1,256,6144]{2,1,0:T(8,128)(2,1)S(1)}, f32[1,16,256]{2,1,0:T(8,128)S(1)}, f32[1,16,256]{2,1,0:T(8,128)S(1)}) custom-call(s32[1]{0:T(128)S(6)} %copy.14.refs_0_, f32[96]{0:T(128)S(1)} %copy-done.4, bf16[1,256,6144]{2,1,0:T(8,128)(2,1)} %refs_2_.1, bf16[1,256,6144]{2,1,0:T(8,128)(2,1)} %refs_3_.1, f32[1,96,256]{2,1,0:T(8,128)S(1)} %copy-done, ...), custom_call_target="tpu_custom_call" | custom-call | tf_op jit(solution)/shard_map/pallas_call | solution.py:350
  45.2 1.7 %copy.15 = bf16[1,256,6144]{2,1,0:T(8,128)(2,1)} copy(bf16[1,256,6144]{2,1,0:T(8,128)(2,1)S(1)} %get-tuple-element.6) | data formatting | bytes 6291456
  46.9 0.6 %copy.16 = f32[1,16,256]{2,1,0:T(8,128)} copy(f32[1,16,256]{2,1,0:T(8,128)S(1)} %get-tuple-element.7) | data formatting | bytes 32768
  47.5 0.6 %copy.17 = f32[1,16,256]{2,1,0:T(8,128)} copy(f32[1,16,256]{2,1,0:T(8,128)S(1)} %get-tuple-element.8) | data formatting | bytes 32768
Async XLA Ops:
  1.3 0.9 %copy-start = (f32[1,96,256]{2,1,0:T(8,128)S(1)}, f32[1,96,256]{2,1,0:T(8,128)}, u32[]{:S(2)}) copy-start(f32[1,96,256]{2,1,0:T(8,128)} %refs_4_.1) | copy-start | bytes 294916
  2.2 0.9 %copy-start.1 = (f32[1,96,256]{2,1,0:T(8,128)S(1)}, f32[1,96,256]{2,1,0:T(8,128)}, u32[]{:S(2)}) copy-start(f32[1,96,256]{2,1,0:T(8,128)} %refs_5_.1) | copy-start | bytes 294916
  3.1 0.7 %copy-start.2 = (bf16[1,16,256]{2,1,0:T(8,128)(2,1)S(1)}, bf16[1,16,256]{2,1,0:T(8,128)(2,1)}, u32[]{:S(2)}) copy-start(bf16[1,16,256]{2,1,0:T(8,128)(2,1)} %refs_6_.1) | copy-start | bytes 24580
  3.8 0.7 %copy-start.3 = (bf16[1,16,256]{2,1,0:T(8,128)(2,1)S(1)}, bf16[1,16,256]{2,1,0:T(8,128)(2,1)}, u32[]{:S(2)}) copy-start(bf16[1,16,256]{2,1,0:T(8,128)(2,1)} %refs_7_.1) | copy-start | bytes 24580
  4.5 0.7 %copy-start.4 = (f32[96]{0:T(128)S(1)}, f32[96]{0:T(128)}, u32[]{:S(2)}) copy-start(f32[96]{0:T(128)} %refs_1_.1) | copy-start | bytes 1156

commit v2 on v1

--- a/solution.py
+++ b/solution.py
@@ -18,7 +18,7 @@
 GROUPS = 16
 PEERS = 32
 LOAD_CHUNKS = 4
-FIRST_WINDOW = 9
+FIRST_WINDOW = 14
 NT = (((1,), (1,)), ((), ()))
 
 
@@ -34,16 +34,21 @@
     scale_b,
     scale_c,
     length_ref,
-    skip_ref,
+    skip_hbm,
     x_hbm,
     dy_hbm,
+    dt_hbm,
+    decay_hbm,
+    b_hbm,
+    c_hbm,
+    gx_ref,
+    gb_ref,
+    gc_ref,
+    skip_ref,
     dt_ref,
     decay_ref,
     b_ref,
     c_ref,
-    gx_ref,
-    gb_ref,
-    gc_ref,
     xv,
     dyv,
     partial_x,
@@ -63,13 +68,41 @@
     states_in,
     load_x_sem,
     load_dy_sem,
+    load_sem,
     sems,
+    state_sem,
 ):
     me = lax.axis_index("seq")
     lane_of_batch = lax.axis_index("batch")
 
     def peer(k):
         return lax.rem(me + k, PEERS)
+
+    my_z = me // 4
+    my_x = lax.rem(me, 4)
+
+    def device_at(dz, dx):
+        return lax.rem(my_z + dz + 8, 8) * 4 + lax.rem(my_x + dx + 4, 4)
+
+    offsets = sorted(
+        ((dz, dx) for dz in range(-3, 5) for dx in range(-1, 3) if (dz, dx) != (0, 0)),
+        key=lambda o: (-abs(o[0]) - abs(o[1]), abs(o[0]), o),
+    )
+
+    small = [
+        pltpu.make_async_copy(source, target, load_sem.at[i])
+        for i, (source, target) in enumerate(
+            (
+                (decay_hbm, decay_ref),
+                (dt_hbm, dt_ref),
+                (b_hbm, b_ref),
+                (c_hbm, c_ref),
+                (skip_hbm, skip_ref),
+            )
+        )
+    ]
+    for copy in small:
+        copy.start()
 
     chunk = 6144 // LOAD_CHUNKS
     loads_x, loads_dy = [], []
@@ -93,6 +126,8 @@
 
     lax.fori_loop(1, PEERS, greet, 0)
 
+    for copy in small:
+        copy.wait()
     decay = decay_ref[0]
     dt = dt_ref[0]
     rows = lax.broadcasted_iota(jnp.int32, (SPAN, SPAN), 0)
@@ -150,6 +185,16 @@
             )
         return carry
 
+    def copy_ends(j):
+        return pltpu.make_async_remote_copy(
+            src_ref=ends_out,
+            dst_ref=ends_in.at[me],
+            send_sem=sems.at[2],
+            recv_sem=sems.at[3],
+            device_id=(j, lane_of_batch),
+            device_id_type=MESH,
+        )
+
     per_chunk = GROUPS // LOAD_CHUNKS
     for i in range(LOAD_CHUNKS):
         loads_x[i].wait()
@@ -168,22 +213,12 @@
             device_id_type=MESH,
         )
 
-    def copy_ends(j):
-        return pltpu.make_async_remote_copy(
-            src_ref=ends_out,
-            dst_ref=ends_in.at[me],
-            send_sem=sems.at[2],
-            recv_sem=sems.at[3],
-            device_id=(j, lane_of_batch),
-            device_id_type=MESH,
-        )
-
     def copy_states(j):
         return pltpu.make_async_remote_copy(
             src_ref=states_out.at[j],
             dst_ref=states_in.at[me],
             send_sem=sems.at[4],
-            recv_sem=sems.at[5],
+            recv_sem=state_sem.at[me],
             device_id=(j, lane_of_batch),
             device_id_type=MESH,
         )
@@ -198,12 +233,10 @@
             device_id_type=MESH,
         )
 
-    def send_first(k, carry):
-        copy_ends(peer(k)).start()
-        copy_parts(peer(k)).start()
-        return carry
-
-    lax.fori_loop(1, PEERS, send_first, 0)
+    for dz, dx in offsets:
+        copy_ends(device_at(dz, dx)).start()
+    for dz, dx in offsets:
+        copy_parts(device_at(dz, dx)).start()
     parts_in[me] = parts_out[me]
     ends_in[me] = ends_out[...]
 
@@ -285,16 +318,23 @@
         states_out[i] = jnp.concatenate([running, scan_g[i]], axis=0).astype(jnp.bfloat16)
         running = ends_wide[i : i + 1, :] * running + parts_in[i].astype(jnp.float32)[:8]
 
-    def send_second(k, carry):
-        copy_states(peer(k)).start()
-        return carry
-
-    lax.fori_loop(1, PEERS, send_second, 0)
+    for dz, dx in offsets:
+        copy_states(device_at(dz, dx)).start()
     states_in[me] = states_out[me]
 
     lax.fori_loop(FIRST_WINDOW, GROUPS, within, 0)
 
-    all_of(states_out, states_in, 4, 5).wait_recv()
+    def await_states(j):
+        @pl.when(j != me)
+        def _():
+            pltpu.make_async_remote_copy(
+                src_ref=states_out.at[j],
+                dst_ref=states_in.at[j],
+                send_sem=sems.at[4],
+                recv_sem=state_sem.at[j],
+                device_id=(peer(1), lane_of_batch),
+                device_id_type=MESH,
+            ).wait_recv()
 
     def spread(rows16):
         blocks = []
@@ -305,8 +345,13 @@
             blocks.append(jnp.concatenate(pad, axis=1))
         return jnp.concatenate(blocks, axis=0)
 
-    def across(g, carry):
+    def across(i, carry):
         cross_b, cross_c = carry
+        order = i // 2
+        away = 4 + ((order + 1) // 2) * (2 * lax.rem(order, 2) - 1)
+        g = lax.rem(my_z + away, 8) * 2 + lax.rem(my_x // 2 + 1 + i, 2)
+        await_states(2 * g)
+        await_states(2 * g + 1)
         lanes = lanes_of(g)
         even = states_in[2 * g].astype(jnp.float32)
         odd = states_in[2 * g + 1].astype(jnp.float32)
@@ -335,7 +380,29 @@
 
     all_of(parts_out, parts_in, 0, 1).wait_send()
     all_of(ends_in, ends_in, 2, 3).wait_send()
-    all_of(states_out, states_in, 4, 5).wait_send()
+    pltpu.make_async_remote_copy(
+        src_ref=states_out.at[pl.ds(0, PEERS - 1)],
+        dst_ref=states_in.at[pl.ds(0, PEERS - 1)],
+        send_sem=sems.at[4],
+        recv_sem=state_sem.at[me],
+        device_id=(peer(1), lane_of_batch),
+        device_id_type=MESH,
+    ).wait_send()
+
+
+def store_results(gx_ref, gb_ref, gc_ref, gx_hbm, gb_hbm, gc_hbm, sem):
+    copies = []
+    for i in range(8):
+        part = pl.ds(32 * i, 32)
+        copies.append(
+            pltpu.make_async_copy(gx_ref.at[0, part], gx_hbm.at[0, part], sem.at[i])
+        )
+    copies.append(pltpu.make_async_copy(gb_ref, gb_hbm, sem.at[8]))
+    copies.append(pltpu.make_async_copy(gc_ref, gc_hbm, sem.at[9]))
+    for copy in copies:
+        copy.start()
+    for copy in copies:
+        copy.wait()
 
 
 def solution(mesh):
@@ -344,19 +411,24 @@
         scale_b = 1.0 / math.sqrt(columns)
         scale_c = math.sqrt(STATE / (columns * PEERS * SPAN))
         vmem = pl.BlockSpec(memory_space=pltpu.VMEM)
-        smem = pl.BlockSpec(memory_space=pltpu.SMEM)
-        whole = pl.BlockSpec(memory_space=pl.ANY)
+        whole = pl.BlockSpec(memory_space=pltpu.HBM)
         f32, bf16 = jnp.float32, jnp.bfloat16
-        return pl.pallas_call(
+        shapes = (
+            jax.ShapeDtypeStruct(inputs.shape, bf16),
+            jax.ShapeDtypeStruct(b_matrix.shape, f32),
+            jax.ShapeDtypeStruct(c_matrix.shape, f32),
+        )
+        results = pl.pallas_call(
             lambda *refs: kernel(scale_b, scale_c, *refs),
-            out_shape=(
-                jax.ShapeDtypeStruct(inputs.shape, bf16),
-                jax.ShapeDtypeStruct(b_matrix.shape, f32),
-                jax.ShapeDtypeStruct(c_matrix.shape, f32),
-            ),
-            in_specs=[smem, smem, whole, whole, vmem, vmem, vmem, vmem],
+            out_shape=tuple(pltpu.VMEM(shape.shape, shape.dtype) for shape in shapes),
+            in_specs=[pl.BlockSpec(memory_space=pltpu.SMEM)] + [whole] * 7,
             out_specs=(vmem, vmem, vmem),
             scratch_shapes=[
+                pltpu.SMEM((96,), f32),
+                pltpu.VMEM((1, 96, SPAN), f32),
+                pltpu.VMEM((1, 96, SPAN), f32),
+                pltpu.VMEM((1, STATE, SPAN), bf16),
+                pltpu.VMEM((1, STATE, SPAN), bf16),
                 pltpu.VMEM((SPAN, columns), bf16),
                 pltpu.VMEM((SPAN, columns), bf16),
                 pltpu.VMEM((SPAN, columns), f32),
@@ -377,11 +449,34 @@
                 pltpu.SemaphoreType.DMA((LOAD_CHUNKS,)),
                 pltpu.SemaphoreType.DMA((LOAD_CHUNKS,)),
                 pltpu.SemaphoreType.DMA((6,)),
+                pltpu.SemaphoreType.DMA((5,)),
+                pltpu.SemaphoreType.DMA((PEERS,)),
             ],
             compiler_params=pltpu.CompilerParams(
                 collective_id=0, has_side_effects=True, vmem_limit_bytes=48 * 1024 * 1024
             ),
-        )(lengths, skip_gain, inputs, out_grad, step_size, log_decay, b_matrix, c_matrix)
+        )(
+            lengths,
+            *(
+                pltpu.with_memory_space_constraint(operand, pltpu.HBM)
+                for operand in (
+                    skip_gain,
+                    inputs,
+                    out_grad,
+                    step_size,
+                    log_decay,
+                    b_matrix,
+                    c_matrix,
+                )
+            )
+        )
+        return pl.pallas_call(
+            store_results,
+            out_shape=shapes,
+            in_specs=[vmem] * 3,
+            out_specs=(whole,) * 3,
+            scratch_shapes=[pltpu.SemaphoreType.DMA((10,))],
+        )(*(pltpu.with_memory_space_constraint(result, pltpu.VMEM) for result in results))
 
     return jax.shard_map(
         local,

time: 48.3 us -> 41.6 us (0.86)
  local copies, waits for them, and re-layouts: 6.7 us -> 0 us
    unnamed x13 -> x0, local copies, waits for them, and re-layouts: 6.7 us -> none
    pallas_call x1 -> x2, Pallas kernels: 40.1 us -> 40.2 us  [the longest x1 38.5 us: local(): pl.pallas_call(lambda *refs: kernel(scale_b, scale_c, *refs), out_shape=t...]
where the time goes in v2:
time: 41.6 us; the launch traced here: 41.5 us
  Pallas kernels  40.2 us (97%)
  between operations  1.29 us (3%)
    pallas_call x1, Pallas kernels, local(): pl.pallas_call(lambda *refs: kernel(scale_b, scale_c, *refs), out_shape=t...  38.5 us
    pallas_call x1, Pallas kernels, local(): pl.pallas_call(store_results, out_shape=shapes, in_specs=[vmem] * 3, out_...  1.74 us

profile of v2, /device:TPU:16, one launch (start us, length us, event | category | flops | bytes accessed | tf_op | source)
XLA Modules:
  0.0 41.5 jit_solution(4602702687454376648)
XLA Ops:
  1.3 38.5 %shard_map.103 = (bf16[1,256,6144]{2,1,0:T(8,128)(2,1)S(1)}, f32[1,16,256]{2,1,0:T(8,128)S(1)}, f32[1,16,256]{2,1,0:T(8,128)S(1)}) custom-call(s32[1]{0:T(128)S(6)} %copy.11.refs_0_, f32[96]{0:T(128)} %refs_1_.1, bf16[1,256,6144]{2,1,0:T(8,128)(2,1)} %refs_2_.1, bf16[1,256,6144]{2,1,0:T(8,128)(2,1)} %refs_3_.1, f32[1,96,256]{2,1,0:T(8,128)} %refs_4_.1, ...), custom_call_target="tpu_custom_call" | custom-call | tf_op jit(solution)/shard_map/pallas_call | solution.py:421
  39.8 1.7 %shard_map.104 = (bf16[1,256,6144]{2,1,0:T(8,128)(2,1)}, f32[1,16,256]{2,1,0:T(8,128)}, f32[1,16,256]{2,1,0:T(8,128)}) custom-call(bf16[1,256,6144]{2,1,0:T(8,128)(2,1)S(1)} %get-tuple-element.6.gx_ref, f32[1,16,256]{2,1,0:T(8,128)S(1)} %get-tuple-element.7.gb_ref, f32[1,16,256]{2,1,0:T(8,128)S(1)} %get-tuple-element.8.gc_ref), custom_call_target="tpu_custom_call" | custom-call | tf_op jit(solution)/shard_map/pallas_call | solution.py:473

commit v3 on v2

--- a/solution.py
+++ b/solution.py
@@ -18,7 +18,11 @@
 GROUPS = 16
 PEERS = 32
 LOAD_CHUNKS = 4
-FIRST_WINDOW = 14
+ROWS = 4
+COLUMNS = 8
+CHUNKS = 3
+QUARTER = 1536
+FILL = (2, 2, 0, 1, 1, 1, 2, 2, 1, 2, 2, 0)
 NT = (((1,), (1,)), ((), ()))
 
 
@@ -62,32 +66,40 @@
     parts_in,
     ends_out,
     ends_in,
-    scan_g,
-    ends_wide,
+    inside,
+    totals_out,
+    totals_in,
+    quad_out,
+    quad_in,
+    before_out,
+    before_in,
     states_out,
     states_in,
     load_x_sem,
     load_dy_sem,
     load_sem,
-    sems,
-    state_sem,
+    send_sem,
+    recv_sem,
 ):
     me = lax.axis_index("seq")
     lane_of_batch = lax.axis_index("batch")
 
-    def peer(k):
-        return lax.rem(me + k, PEERS)
-
-    my_z = me // 4
-    my_x = lax.rem(me, 4)
-
-    def device_at(dz, dx):
-        return lax.rem(my_z + dz + 8, 8) * 4 + lax.rem(my_x + dx + 4, 4)
-
-    offsets = sorted(
-        ((dz, dx) for dz in range(-3, 5) for dx in range(-1, 3) if (dz, dx) != (0, 0)),
-        key=lambda o: (-abs(o[0]) - abs(o[1]), abs(o[0]), o),
-    )
+    my_z = me // ROWS
+    my_x = lax.rem(me, ROWS)
+    row_offsets = (2, 1, 3)
+    column_offsets = (4, 3, 5, 2, 6, 1, 7)
+
+    def row_peer(dx):
+        return lax.rem(my_x + dx, ROWS)
+
+    def column_peer(dz):
+        return lax.rem(my_z + dz, COLUMNS)
+
+    def row_device(dx):
+        return (my_z * ROWS + row_peer(dx), lane_of_batch)
+
+    def column_device(dz):
+        return (column_peer(dz) * ROWS + my_x, lane_of_batch)
 
     small = [
         pltpu.make_async_copy(source, target, load_sem.at[i])
@@ -118,13 +130,10 @@
 
     barrier = pltpu.get_barrier_semaphore()
 
-    def greet(k, carry):
-        pl.semaphore_signal(
-            barrier, inc=1, device_id=(peer(k), lane_of_batch), device_id_type=MESH
-        )
-        return carry
-
-    lax.fori_loop(1, PEERS, greet, 0)
+    for dx in row_offsets:
+        pl.semaphore_signal(barrier, inc=1, device_id=row_device(dx), device_id_type=MESH)
+    for dz in column_offsets:
+        pl.semaphore_signal(barrier, inc=1, device_id=column_device(dz), device_id_type=MESH)
 
     for copy in small:
         copy.wait()
@@ -145,7 +154,22 @@
         from_start_s[g, 0:HEADS_PER_GROUP, :] = from_start[take]
     padded = jnp.concatenate([decay, jnp.zeros((32, SPAN), jnp.float32)], axis=0)
     total = nt_dot(jnp.ones((8, SPAN), jnp.float32), padded, HIGHEST)
-    ends_out[...] = jnp.exp(total[0:1])
+    ends = jnp.exp(total[0:1])
+    ends_high = ends.astype(jnp.bfloat16)
+    rest = ends - ends_high.astype(jnp.float32)
+    ends_mid = rest.astype(jnp.bfloat16)
+    ends_low = rest - ends_mid.astype(jnp.float32)
+    split_ends = jnp.concatenate(
+        [
+            ends_high.astype(jnp.float32),
+            ends_mid.astype(jnp.float32),
+            ends_low,
+            jnp.zeros((13, HALF), jnp.float32),
+        ],
+        axis=0,
+    ).astype(jnp.bfloat16)
+    head_row = lax.broadcasted_iota(jnp.int32, (HALF, LANES), 0)
+    lane_head = lax.broadcasted_iota(jnp.int32, (HALF, LANES), 1) // 64
     b_wide = b_ref[0].astype(jnp.float32)
     c_wide = c_ref[0].astype(jnp.float32)
     b_turned = jnp.transpose(b_wide).astype(jnp.bfloat16)
@@ -180,20 +204,15 @@
         grad = own_heads(plain_dot(per_head(c_wide, from_start_s[g]), dy))
         for half in range(2):
             take = slice(8 * half, 8 * half + 8)
-            parts_out[2 * g + half] = jnp.concatenate([state[take], grad[take]], axis=0).astype(
-                jnp.bfloat16
-            )
+            both = jnp.concatenate([state[take], grad[take]], axis=0).astype(jnp.bfloat16)
+            for c in range(CHUNKS):
+                parts_out[c, g // 4, 2 * lax.rem(g, 4) + half] = both[:, HALF * c : HALF * c + HALF]
+        pick = (head_row == lane_head + g * HEADS_PER_GROUP).astype(jnp.float32)
+        wide = plain_dot(split_ends, pick.astype(jnp.bfloat16))
+        ends_out[g // 4, :, pl.ds(pl.multiple_of(lax.rem(g, 4) * LANES, HALF), LANES)] = (
+            wide[0:1] + wide[1:2] + wide[2:3]
+        )
         return carry
-
-    def copy_ends(j):
-        return pltpu.make_async_remote_copy(
-            src_ref=ends_out,
-            dst_ref=ends_in.at[me],
-            send_sem=sems.at[2],
-            recv_sem=sems.at[3],
-            device_id=(j, lane_of_batch),
-            device_id_type=MESH,
-        )
 
     per_chunk = GROUPS // LOAD_CHUNKS
     for i in range(LOAD_CHUNKS):
@@ -201,44 +220,38 @@
         loads_dy[i].wait()
         lax.fori_loop(i * per_chunk, (i + 1) * per_chunk, summary, 0)
 
-    pl.semaphore_wait(barrier, PEERS - 1)
-
-    def copy_parts(j):
+    pl.semaphore_wait(barrier, ROWS + COLUMNS - 2)
+
+    def remote(source, target, slot, device):
         return pltpu.make_async_remote_copy(
-            src_ref=parts_out.at[j],
-            dst_ref=parts_in.at[me],
-            send_sem=sems.at[0],
-            recv_sem=sems.at[1],
-            device_id=(j, lane_of_batch),
+            src_ref=source,
+            dst_ref=target,
+            send_sem=send_sem.at[slot],
+            recv_sem=recv_sem.at[slot],
+            device_id=device,
             device_id_type=MESH,
         )
 
-    def copy_states(j):
-        return pltpu.make_async_remote_copy(
-            src_ref=states_out.at[j],
-            dst_ref=states_in.at[me],
-            send_sem=sems.at[4],
-            recv_sem=state_sem.at[me],
-            device_id=(j, lane_of_batch),
-            device_id_type=MESH,
-        )
-
-    def all_of(out_ref, in_ref, send, recv):
-        return pltpu.make_async_remote_copy(
-            src_ref=out_ref.at[pl.ds(0, PEERS - 1)],
-            dst_ref=in_ref.at[pl.ds(0, PEERS - 1)],
-            send_sem=sems.at[send],
-            recv_sem=sems.at[recv],
-            device_id=(peer(1), lane_of_batch),
-            device_id_type=MESH,
-        )
-
-    for dz, dx in offsets:
-        copy_ends(device_at(dz, dx)).start()
-    for dz, dx in offsets:
-        copy_parts(device_at(dz, dx)).start()
-    parts_in[me] = parts_out[me]
-    ends_in[me] = ends_out[...]
+    def row_wait(out_ref, in_ref, slot):
+        few = pl.ds(0, ROWS - 1)
+        return remote(out_ref.at[few], in_ref.at[few], slot, row_device(1))
+
+    def column_wait(out_ref, in_ref, slot):
+        few = pl.ds(0, COLUMNS - 1)
+        return remote(out_ref.at[few], in_ref.at[few], slot, column_device(1))
+
+    for dx in row_offsets:
+        remote(ends_out.at[row_peer(dx)], ends_in.at[my_x], 12, row_device(dx)).start()
+    def send_parts(c):
+        for dx in row_offsets:
+            remote(
+                parts_out.at[c, row_peer(dx)], parts_in.at[c, my_x], c, row_device(dx)
+            ).start()
+
+    send_parts(0)
+    for c in range(CHUNKS):
+        parts_in[c, my_x] = parts_out[c, my_x]
+    ends_in[my_x] = ends_out[my_x]
 
     causal = lax.broadcasted_iota(jnp.int32, (HALF, HALF), 0) <= lax.broadcasted_iota(
         jnp.int32, (HALF, HALF), 1
@@ -298,96 +311,181 @@
         mix_s[HALF:, HALF:] += mix_bb
         return carry
 
-    lax.fori_loop(0, FIRST_WINDOW, within, 0)
-
-    all_of(parts_out, parts_in, 0, 1).wait_recv()
-    all_of(ends_in, ends_in, 2, 3).wait_recv()
-
-    head_row = lax.broadcasted_iota(jnp.int32, (HALF, LANES), 0)
-    lane_head = lax.broadcasted_iota(jnp.int32, (HALF, LANES), 1) // 64
-    mine = (head_row == lane_head + (me // 2) * HEADS_PER_GROUP).astype(jnp.float32)
-    gathered = jnp.concatenate([ends_in[i] for i in range(PEERS)], axis=0)
-    ends_wide[...] = plain_dot(gathered, mine, HIGHEST)
-
-    running = jnp.zeros((8, LANES), jnp.float32)
-    for i in reversed(range(PEERS)):
-        scan_g[i] = running
-        running = ends_wide[i : i + 1, :] * running + parts_in[i].astype(jnp.float32)[8:]
-    running = jnp.zeros((8, LANES), jnp.float32)
-    for i in range(PEERS):
-        states_out[i] = jnp.concatenate([running, scan_g[i]], axis=0).astype(jnp.bfloat16)
-        running = ends_wide[i : i + 1, :] * running + parts_in[i].astype(jnp.float32)[:8]
-
-    for dz, dx in offsets:
-        copy_states(device_at(dz, dx)).start()
-    states_in[me] = states_out[me]
-
-    lax.fori_loop(FIRST_WINDOW, GROUPS, within, 0)
-
-    def await_states(j):
-        @pl.when(j != me)
-        def _():
-            pltpu.make_async_remote_copy(
-                src_ref=states_out.at[j],
-                dst_ref=states_in.at[j],
-                send_sem=sems.at[4],
-                recv_sem=state_sem.at[j],
-                device_id=(peer(1), lane_of_batch),
-                device_id_type=MESH,
-            ).wait_recv()
-
-    def spread(rows16):
-        blocks = []
-        for k in range(3):
-            tile = rows16[:, HALF * k : HALF * k + HALF]
-            pad = [jnp.zeros((32, HALF), jnp.bfloat16)] * 3
-            pad[k] = jnp.concatenate([tile * keep[0], tile * keep[1]], axis=0)
-            blocks.append(jnp.concatenate(pad, axis=1))
-        return jnp.concatenate(blocks, axis=0)
-
-    def across(i, carry):
+    fills = list(FILL)
+    done = [0]
+
+    def fill():
+        count = fills.pop(0)
+        lax.fori_loop(done[0], done[0] + count, within, 0)
+        done[0] += count
+
+    def decay_rows(z, c):
+        lanes = slice(LANES * (z // 2) + HALF * c, LANES * (z // 2) + HALF * c + HALF)
+        return [ends_in[x, :, lanes] for x in range(ROWS)]
+
+    def join_row(c):
+        row_wait(parts_out.at[c], parts_in.at[c], c).wait_recv()
+        if c == 0:
+            row_wait(ends_out, ends_in, 12).wait_recv()
+            quad = ends_in[0] * ends_in[1] * ends_in[2] * ends_in[3]
+            for k in range(4):
+                quad_out[k] = quad[:, LANES * k : LANES * k + LANES]
+        for z in range(COLUMNS):
+            decays = decay_rows(z, c)
+            parts = [parts_in[c, x, z].astype(jnp.float32) for x in range(ROWS)]
+            state = jnp.zeros((8, HALF), jnp.float32)
+            states = []
+            for x in range(ROWS):
+                states.append(state)
+                state = decays[x] * state + parts[x][:8]
+            grad = jnp.zeros((8, HALF), jnp.float32)
+            grads = [None] * ROWS
+            for x in reversed(range(ROWS)):
+                grads[x] = grad
+                grad = decays[x] * grad + parts[x][8:]
+            totals_out[c, z] = jnp.concatenate([state, grad], axis=0).astype(jnp.bfloat16)
+            for x in range(ROWS):
+                inside[c, x, z] = jnp.concatenate([states[x], grads[x]], axis=0)
+        if c == 0:
+            for dz in column_offsets:
+                remote(
+                    quad_out.at[column_peer(dz) // 2], quad_in.at[my_z], 13, column_device(dz)
+                ).start()
+            quad_in[my_z] = quad_out[my_z // 2]
+        for dz in column_offsets:
+            remote(
+                totals_out.at[c, column_peer(dz)],
+                totals_in.at[c, my_z],
+                3 + c,
+                column_device(dz),
+            ).start()
+        totals_in[c, my_z] = totals_out[c, my_z]
+
+    def scan_column(c):
+        column_wait(totals_out.at[c], totals_in.at[c], 3 + c).wait_recv()
+        if c == 0:
+            column_wait(quad_in, quad_in, 13).wait_recv()
+        decays = [quad_in[z, :, HALF * c : HALF * c + HALF] for z in range(COLUMNS)]
+        parts = [totals_in[c, z].astype(jnp.float32) for z in range(COLUMNS)]
+        state = jnp.zeros((8, HALF), jnp.float32)
+        states = []
+        for z in range(COLUMNS):
+            states.append(state)
+            state = decays[z] * state + parts[z][:8]
+        grad = jnp.zeros((8, HALF), jnp.float32)
+        for z in reversed(range(COLUMNS)):
+            before_out[c, z] = jnp.concatenate([states[z], grad], axis=0).astype(jnp.bfloat16)
+            grad = decays[z] * grad + parts[z][8:]
+        for dz in column_offsets:
+            remote(
+                before_out.at[c, column_peer(dz)],
+                before_in.at[c, my_z],
+                6 + c,
+                column_device(dz),
+            ).start()
+        before_in[c, my_z] = before_out[c, my_z]
+
+    def finish_row(c):
+        column_wait(before_out.at[c], before_in.at[c], 6 + c).wait_recv()
+        for z in range(COLUMNS):
+            decays = decay_rows(z, c)
+            outside = before_in[c, z].astype(jnp.float32)
+            state = outside[:8]
+            states = []
+            for x in range(ROWS):
+                states.append(state)
+                if x < ROWS - 1:
+                    state = decays[x] * state
+            grad = outside[8:]
+            for x in reversed(range(ROWS)):
+                entering = jnp.concatenate([states[x], grad], axis=0) + inside[c, x, z]
+                states_out[c, x, z] = entering.astype(jnp.bfloat16)
+                if x > 0:
+                    grad = decays[x] * grad
+        for dx in row_offsets:
+            remote(
+                states_out.at[c, row_peer(dx)], states_in.at[c, my_x], 9 + c, row_device(dx)
+            ).start()
+        states_in[c, my_x] = states_out[c, my_x]
+
+    for c in range(1, CHUNKS):
+        fill()
+        send_parts(c)
+    for stage in (join_row, scan_column, finish_row):
+        for c in range(CHUNKS):
+            fill()
+            stage(c)
+    fill()
+
+    def turned_rows(c, g):
+        first = states_in[c, g // 4, 2 * lax.rem(g, 4)].astype(jnp.float32)
+        second = states_in[c, g // 4, 2 * lax.rem(g, 4) + 1].astype(jnp.float32)
+        return (
+            jnp.concatenate([first[:8], second[:8]], axis=0).astype(jnp.bfloat16),
+            jnp.concatenate([first[8:], second[8:]], axis=0).astype(jnp.bfloat16),
+        )
+
+    def spread(one, two):
+        blank = jnp.zeros((2 * STATE, HALF), jnp.bfloat16)
+        top = jnp.concatenate([one * keep[0], one * keep[1]], axis=0)
+        bottom = jnp.concatenate([two * keep[0], two * keep[1]], axis=0)
+        return jnp.concatenate(
+            [
+                jnp.concatenate([top, blank], axis=1),
+                jnp.concatenate([blank, bottom], axis=1),
+            ],
+            axis=0,
+        )
+
+    def across(c, pair, carry):
         cross_b, cross_c = carry
-        order = i // 2
-        away = 4 + ((order + 1) // 2) * (2 * lax.rem(order, 2) - 1)
-        g = lax.rem(my_z + away, 8) * 2 + lax.rem(my_x // 2 + 1 + i, 2)
-        await_states(2 * g)
-        await_states(2 * g + 1)
-        lanes = lanes_of(g)
-        even = states_in[2 * g].astype(jnp.float32)
-        odd = states_in[2 * g + 1].astype(jnp.float32)
-        state = spread(jnp.concatenate([even[:8], odd[:8]], axis=0).astype(jnp.bfloat16))
-        grad = spread(jnp.concatenate([even[8:], odd[8:]], axis=0).astype(jnp.bfloat16))
-        ends = to_end_s[g]
-        starts = from_start_s[g]
-        into = jnp.concatenate(
-            [b_wide * ends[k : k + 1, :] for k in range(HEADS_PER_GROUP)], axis=0
-        )
+        groups = (2 * pair, 2 * pair + 1)
+        lanes = [pl.ds(pl.multiple_of(g * LANES + HALF * c, HALF), HALF) for g in groups]
+        state_one, grad_one = turned_rows(c, groups[0])
+        state_two, grad_two = turned_rows(c, groups[1])
+        state = spread(state_one, state_two)
+        grad = spread(grad_one, grad_two)
+        heads = slice(2 * c, 2 * c + 2)
+        ends = jnp.concatenate([to_end_s[g][heads] for g in groups], axis=0)
+        starts = jnp.concatenate([from_start_s[g][heads] for g in groups], axis=0)
+        into = jnp.concatenate([b_wide * ends[k : k + 1, :] for k in range(4)], axis=0)
         term = plain_dot(jnp.transpose(into).astype(jnp.bfloat16), grad)
-        gx_ref[0, :, lanes] = (partial_x[:, lanes] + term).astype(jnp.bfloat16)
-        from_x = nt_dot(grad, xv[:, lanes])
-        from_dy = nt_dot(state, dyv[:, lanes])
-        for k in range(HEADS_PER_GROUP):
+        for k in range(2):
+            gx_ref[0, :, lanes[k]] = (
+                partial_x[:, lanes[k]] + term[:, HALF * k : HALF * k + HALF]
+            ).astype(jnp.bfloat16)
+        x = jnp.concatenate([xv[:, part] for part in lanes], axis=1)
+        dy = jnp.concatenate([dyv[:, part] for part in lanes], axis=1)
+        from_x = nt_dot(grad, x)
+        from_dy = nt_dot(state, dy)
+        for k in range(4):
             take = slice(STATE * k, STATE * k + STATE)
             cross_b += from_x[take] * ends[k : k + 1, :]
             cross_c += from_dy[take] * starts[k : k + 1, :]
         return cross_b, cross_c
 
     zero = jnp.zeros((STATE, SPAN), jnp.float32)
-    cross_b, cross_c = lax.fori_loop(0, GROUPS, across, (zero, zero))
+    crosses = (zero, zero)
+    for c in range(CHUNKS):
+        row_wait(states_out.at[c], states_in.at[c], 9 + c).wait_recv()
+        crosses = lax.fori_loop(
+            0,
+            GROUPS // 4,
+            lambda two, carry, c=c: across(c, 2 * two + 1, across(c, 2 * two, carry)),
+            crosses,
+        )
+    cross_b, cross_c = crosses
     mixing = mix_s[...]
     gb_ref[0] = (nt_dot(c_wide, mixing, HIGHEST) + cross_b) * scale_b
     gc_ref[0] = (plain_dot(b_wide, mixing, HIGHEST) + cross_c) * scale_c
 
-    all_of(parts_out, parts_in, 0, 1).wait_send()
-    all_of(ends_in, ends_in, 2, 3).wait_send()
-    pltpu.make_async_remote_copy(
-        src_ref=states_out.at[pl.ds(0, PEERS - 1)],
-        dst_ref=states_in.at[pl.ds(0, PEERS - 1)],
-        send_sem=sems.at[4],
-        recv_sem=state_sem.at[me],
-        device_id=(peer(1), lane_of_batch),
-        device_id_type=MESH,
-    ).wait_send()
+    for c in range(CHUNKS):
+        row_wait(parts_out.at[c], parts_in.at[c], c).wait_send()
+        column_wait(totals_out.at[c], totals_in.at[c], 3 + c).wait_send()
+        column_wait(before_out.at[c], before_in.at[c], 6 + c).wait_send()
+        row_wait(states_out.at[c], states_in.at[c], 9 + c).wait_send()
+    row_wait(ends_out, ends_in, 12).wait_send()
+    column_wait(quad_in, quad_in, 13).wait_send()
 
 
 def store_results(gx_ref, gb_ref, gc_ref, gx_hbm, gb_hbm, gc_hbm, sem):
@@ -438,19 +536,24 @@
                 pltpu.VMEM((GROUPS, 8, SPAN), f32),
                 pltpu.VMEM((SPAN, SPAN), f32),
                 pltpu.VMEM((SPAN, SPAN), f32),
-                pltpu.VMEM((PEERS, 16, LANES), bf16),
-                pltpu.VMEM((PEERS, 16, LANES), bf16),
-                pltpu.VMEM((1, HALF), f32),
-                pltpu.VMEM((PEERS, 1, HALF), f32),
-                pltpu.VMEM((PEERS, 8, LANES), f32),
-                pltpu.VMEM((PEERS, LANES), f32),
-                pltpu.VMEM((PEERS, 16, LANES), bf16),
-                pltpu.VMEM((PEERS, 16, LANES), bf16),
+                pltpu.VMEM((CHUNKS, ROWS, COLUMNS, 16, HALF), bf16),
+                pltpu.VMEM((CHUNKS, ROWS, COLUMNS, 16, HALF), bf16),
+                pltpu.VMEM((ROWS, 1, QUARTER), f32),
+                pltpu.VMEM((ROWS, 1, QUARTER), f32),
+                pltpu.VMEM((CHUNKS, ROWS, COLUMNS, 16, HALF), f32),
+                pltpu.VMEM((CHUNKS, COLUMNS, 16, HALF), bf16),
+                pltpu.VMEM((CHUNKS, COLUMNS, 16, HALF), bf16),
+                pltpu.VMEM((4, 1, LANES), f32),
+                pltpu.VMEM((COLUMNS, 1, LANES), f32),
+                pltpu.VMEM((CHUNKS, COLUMNS, 16, HALF), bf16),
+                pltpu.VMEM((CHUNKS, COLUMNS, 16, HALF), bf16),
+                pltpu.VMEM((CHUNKS, ROWS, COLUMNS, 16, HALF), bf16),
+                pltpu.VMEM((CHUNKS, ROWS, COLUMNS, 16, HALF), bf16),
                 pltpu.SemaphoreType.DMA((LOAD_CHUNKS,)),
                 pltpu.SemaphoreType.DMA((LOAD_CHUNKS,)),
-                pltpu.SemaphoreType.DMA((6,)),
                 pltpu.SemaphoreType.DMA((5,)),
-                pltpu.SemaphoreType.DMA((PEERS,)),
+                pltpu.SemaphoreType.DMA((14,)),
+                pltpu.SemaphoreType.DMA((14,)),
             ],
             compiler_params=pltpu.CompilerParams(
                 collective_id=0, has_side_effects=True, vmem_limit_bytes=48 * 1024 * 1024

time: 41.6 us -> 36.1 us (0.87)
  Pallas kernels: 40.2 us -> 34.7 us
    pallas_call x1, Pallas kernels: 38.5 us -> 33 us  [local(): pl.pallas_call(lambda *refs: kernel(scale_b, scale_c, *refs), out_shape=t...]
where the time goes in v3:
time: 36.1 us; the launch traced here: 36 us
  Pallas kernels  34.7 us (96%)
  between operations  1.29 us (4%)
    pallas_call x1, Pallas kernels, local(): pl.pallas_call(lambda *refs: kernel(scale_b, scale_c, *refs), out_shape=t...  33 us
    pallas_call x1, Pallas kernels, local(): pl.pallas_call(store_results, out_shape=shapes, in_specs=[vmem] * 3, out_...  1.74 us

profile of v3, /device:TPU:16, one launch (start us, length us, event | category | flops | bytes accessed | tf_op | source)
XLA Modules:
  0.0 36.0 jit_solution(3399873182098845403)
XLA Ops:
  1.3 33.0 %shard_map.103 = (bf16[1,256,6144]{2,1,0:T(8,128)(2,1)S(1)}, f32[1,16,256]{2,1,0:T(8,128)S(1)}, f32[1,16,256]{2,1,0:T(8,128)S(1)}) custom-call(s32[1]{0:T(128)S(6)} %copy.11.refs_0_, f32[96]{0:T(128)} %refs_1_.1, bf16[1,256,6144]{2,1,0:T(8,128)(2,1)} %refs_2_.1, bf16[1,256,6144]{2,1,0:T(8,128)(2,1)} %refs_3_.1, f32[1,96,256]{2,1,0:T(8,128)} %refs_4_.1, ...), custom_call_target="tpu_custom_call" | custom-call | tf_op jit(solution)/shard_map/pallas_call | solution.py:519
  34.3 1.7 %shard_map.104 = (bf16[1,256,6144]{2,1,0:T(8,128)(2,1)}, f32[1,16,256]{2,1,0:T(8,128)}, f32[1,16,256]{2,1,0:T(8,128)}) custom-call(bf16[1,256,6144]{2,1,0:T(8,128)(2,1)S(1)} %get-tuple-element.6.gx_ref, f32[1,16,256]{2,1,0:T(8,128)S(1)} %get-tuple-element.7.gb_ref, f32[1,16,256]{2,1,0:T(8,128)S(1)} %get-tuple-element.8.gc_ref), custom_call_target="tpu_custom_call" | custom-call | tf_op jit(solution)/shard_map/pallas_call | solution.py:576

commit v4 on v3

--- a/solution.py
+++ b/solution.py
@@ -22,7 +22,7 @@
 COLUMNS = 8
 CHUNKS = 3
 QUARTER = 1536
-FILL = (2, 2, 0, 1, 1, 1, 2, 2, 1, 2, 2, 0)
+FILL = (2, 1, 1, 2, 1, 2, 2, 1, 1, 2, 1)
 NT = (((1,), (1,)), ((), ()))
 
 
@@ -116,10 +116,10 @@
     for copy in small:
         copy.start()
 
-    chunk = 6144 // LOAD_CHUNKS
+    quarters = [row_peer(dx) for dx in row_offsets + (0,)]
     loads_x, loads_dy = [], []
-    for i in range(LOAD_CHUNKS):
-        part = pl.ds(i * chunk, chunk)
+    for i, quarter in enumerate(quarters):
+        part = pl.ds(pl.multiple_of(quarter * QUARTER, HALF), QUARTER)
         loads_x.append(pltpu.make_async_copy(x_hbm.at[0, :, part], xv.at[:, part], load_x_sem.at[i]))
         loads_dy.append(
             pltpu.make_async_copy(dy_hbm.at[0, :, part], dyv.at[:, part], load_dy_sem.at[i])
@@ -214,14 +214,6 @@
         )
         return carry
 
-    per_chunk = GROUPS // LOAD_CHUNKS
-    for i in range(LOAD_CHUNKS):
-        loads_x[i].wait()
-        loads_dy[i].wait()
-        lax.fori_loop(i * per_chunk, (i + 1) * per_chunk, summary, 0)
-
-    pl.semaphore_wait(barrier, ROWS + COLUMNS - 2)
-
     def remote(source, target, slot, device):
         return pltpu.make_async_remote_copy(
             src_ref=source,
@@ -240,15 +232,33 @@
         few = pl.ds(0, COLUMNS - 1)
         return remote(out_ref.at[few], in_ref.at[few], slot, column_device(1))
 
-    for dx in row_offsets:
-        remote(ends_out.at[row_peer(dx)], ends_in.at[my_x], 12, row_device(dx)).start()
+    def send_part(c, dx):
+        remote(
+            parts_out.at[c, row_peer(dx)], parts_in.at[c, my_x], c, row_device(dx)
+        ).start()
+
     def send_parts(c):
         for dx in row_offsets:
-            remote(
-                parts_out.at[c, row_peer(dx)], parts_in.at[c, my_x], c, row_device(dx)
-            ).start()
-
-    send_parts(0)
+            send_part(c, dx)
+
+    for i, quarter in enumerate(quarters):
+        loads_x[i].wait()
+        loads_dy[i].wait()
+        lax.fori_loop(
+            0,
+            2,
+            lambda k, carry, first=4 * quarter: summary(
+                first + 2 * k + 1, summary(first + 2 * k, carry)
+            ),
+            0,
+        )
+        if i == 0:
+            pl.semaphore_wait(barrier, ROWS + COLUMNS - 2)
+        if i < ROWS - 1:
+            dx = row_offsets[i]
+            remote(ends_out.at[quarter], ends_in.at[my_x], 12, row_device(dx)).start()
+            send_part(0, dx)
+    send_parts(1)
     for c in range(CHUNKS):
         parts_in[c, my_x] = parts_out[c, my_x]
     ends_in[my_x] = ends_out[my_x]
@@ -408,14 +418,16 @@
             ).start()
         states_in[c, my_x] = states_out[c, my_x]
 
-    for c in range(1, CHUNKS):
-        fill()
-        send_parts(c)
+    fill()
+    send_parts(2)
     for stage in (join_row, scan_column, finish_row):
         for c in range(CHUNKS):
             fill()
             stage(c)
     fill()
+    mixing = mix_s[...]
+    base_b = nt_dot(c_wide, mixing, HIGHEST)
+    base_c = plain_dot(b_wide, mixing, HIGHEST)
 
     def turned_rows(c, g):
         first = states_in[c, g // 4, 2 * lax.rem(g, 4)].astype(jnp.float32)
@@ -464,8 +476,7 @@
             cross_c += from_dy[take] * starts[k : k + 1, :]
         return cross_b, cross_c
 
-    zero = jnp.zeros((STATE, SPAN), jnp.float32)
-    crosses = (zero, zero)
+    crosses = (base_b, base_c)
     for c in range(CHUNKS):
         row_wait(states_out.at[c], states_in.at[c], 9 + c).wait_recv()
         crosses = lax.fori_loop(
@@ -475,9 +486,8 @@
             crosses,
         )
     cross_b, cross_c = crosses
-    mixing = mix_s[...]
-    gb_ref[0] = (nt_dot(c_wide, mixing, HIGHEST) + cross_b) * scale_b
-    gc_ref[0] = (plain_dot(b_wide, mixing, HIGHEST) + cross_c) * scale_c
+    gb_ref[0] = cross_b * scale_b
+    gc_ref[0] = cross_c * scale_c
 
     for c in range(CHUNKS):
         row_wait(parts_out.at[c], parts_in.at[c], c).wait_send()

time: 36.1 us -> 34.8 us (0.964)
  Pallas kernels: 34.7 us -> 33.4 us
    pallas_call x1, Pallas kernels: 33 us -> 31.7 us  [local(): pl.pallas_call(lambda *refs: kernel(scale_b, scale_c, *refs), out_shape=t...]
where the time goes in v4:
time: 34.8 us; the launch traced here: 34.7 us
  Pallas kernels  33.4 us (96%)
  between operations  1.29 us (4%)
    pallas_call x1, Pallas kernels, local(): pl.pallas_call(lambda *refs: kernel(scale_b, scale_c, *refs), out_shape=t...  31.7 us
    pallas_call x1, Pallas kernels, local(): pl.pallas_call(store_results, out_shape=shapes, in_specs=[vmem] * 3, out_...  1.74 us

profile of v4, /device:TPU:16, one launch (start us, length us, event | category | flops | bytes accessed | tf_op | source)
XLA Modules:
  0.0 34.7 jit_solution(5540982298521314502)
XLA Ops:
  1.3 31.7 %shard_map.103 = (bf16[1,256,6144]{2,1,0:T(8,128)(2,1)S(1)}, f32[1,16,256]{2,1,0:T(8,128)S(1)}, f32[1,16,256]{2,1,0:T(8,128)S(1)}) custom-call(s32[1]{0:T(128)S(6)} %copy.11.refs_0_, f32[96]{0:T(128)} %refs_1_.1, bf16[1,256,6144]{2,1,0:T(8,128)(2,1)} %refs_2_.1, bf16[1,256,6144]{2,1,0:T(8,128)(2,1)} %refs_3_.1, f32[1,96,256]{2,1,0:T(8,128)} %refs_4_.1, ...), custom_call_target="tpu_custom_call" | custom-call | tf_op jit(solution)/shard_map/pallas_call | solution.py:529
  32.9 1.7 %shard_map.104 = (bf16[1,256,6144]{2,1,0:T(8,128)(2,1)}, f32[1,16,256]{2,1,0:T(8,128)}, f32[1,16,256]{2,1,0:T(8,128)}) custom-call(bf16[1,256,6144]{2,1,0:T(8,128)(2,1)S(1)} %get-tuple-element.6.gx_ref, f32[1,16,256]{2,1,0:T(8,128)S(1)} %get-tuple-element.7.gb_ref, f32[1,16,256]{2,1,0:T(8,128)S(1)} %get-tuple-element.8.gc_ref), custom_call_target="tpu_custom_call" | custom-call | tf_op jit(solution)/shard_map/pallas_call | solution.py:586

commit v5 on v4

--- a/solution.py
+++ b/solution.py
@@ -34,9 +34,68 @@
     return jnp.dot(a, b, precision=precision, preferred_element_type=jnp.float32)
 
 
+def lane_masks():
+    lane = lax.broadcasted_iota(jnp.int32, (1, HALF), 1)
+    return (
+        (lane < 64).astype(jnp.float32).astype(jnp.bfloat16),
+        (lane >= 64).astype(jnp.float32).astype(jnp.bfloat16),
+    )
+
+
+def turned_rows(states, g):
+    first = states[g // 4, 2 * lax.rem(g, 4)].astype(jnp.float32)
+    second = states[g // 4, 2 * lax.rem(g, 4) + 1].astype(jnp.float32)
+    return (
+        jnp.concatenate([first[:8], second[:8]], axis=0).astype(jnp.bfloat16),
+        jnp.concatenate([first[8:], second[8:]], axis=0).astype(jnp.bfloat16),
+    )
+
+
+def spread(one, two):
+    low, high = lane_masks()
+    blank = jnp.zeros((2 * STATE, HALF), jnp.bfloat16)
+    top = jnp.concatenate([one * low, one * high], axis=0)
+    bottom = jnp.concatenate([two * low, two * high], axis=0)
+    return jnp.concatenate(
+        [
+            jnp.concatenate([top, blank], axis=1),
+            jnp.concatenate([blank, bottom], axis=1),
+        ],
+        axis=0,
+    )
+
+
+def across(c, pair, carry, states, b_wide, xv, dyv, partial_x, to_end_s, from_start_s, store):
+    cross_b, cross_c = carry
+    groups = (2 * pair, 2 * pair + 1)
+    lanes = [pl.ds(pl.multiple_of(g * LANES + HALF * c, HALF), HALF) for g in groups]
+    state_one, grad_one = turned_rows(states, groups[0])
+    state_two, grad_two = turned_rows(states, groups[1])
+    state = spread(state_one, state_two)
+    grad = spread(grad_one, grad_two)
+    heads = slice(2 * c, 2 * c + 2)
+    ends = jnp.concatenate([to_end_s[g][heads] for g in groups], axis=0)
+    starts = jnp.concatenate([from_start_s[g][heads] for g in groups], axis=0)
+    into = jnp.concatenate([b_wide * ends[k : k + 1, :] for k in range(4)], axis=0)
+    term = plain_dot(jnp.transpose(into).astype(jnp.bfloat16), grad)
+    for k in range(2):
+        store(
+            groups[k],
+            lanes[k],
+            (partial_x[:, lanes[k]] + term[:, HALF * k : HALF * k + HALF]).astype(jnp.bfloat16),
+        )
+    x = jnp.concatenate([xv[:, part] for part in lanes], axis=1)
+    dy = jnp.concatenate([dyv[:, part] for part in lanes], axis=1)
+    from_x = nt_dot(grad, x)
+    from_dy = nt_dot(state, dy)
+    for k in range(4):
+        take = slice(STATE * k, STATE * k + STATE)
+        cross_b += from_x[take] * ends[k : k + 1, :]
+        cross_c += from_dy[take] * starts[k : k + 1, :]
+    return cross_b, cross_c
+
+
 def kernel(
-    scale_b,
-    scale_c,
     length_ref,
     skip_hbm,
     x_hbm,
@@ -46,20 +105,22 @@
     b_hbm,
     c_hbm,
     gx_ref,
-    gb_ref,
-    gc_ref,
+    cross_b_ref,
+    cross_c_ref,
+    xv,
+    dyv,
+    partial_x,
+    to_end_s,
+    from_start_s,
+    b_out,
+    late_states,
     skip_ref,
     dt_ref,
     decay_ref,
     b_ref,
     c_ref,
-    xv,
-    dyv,
-    partial_x,
     row_s,
     col_s,
-    to_end_s,
-    from_start_s,
     cb_s,
     mix_s,
     parts_out,
@@ -267,10 +328,7 @@
         jnp.int32, (HALF, HALF), 1
     )
     lane_row = lax.broadcasted_iota(jnp.int32, (1, HALF), 1)
-    keep = (
-        (lane_row < 64).astype(jnp.float32).astype(jnp.bfloat16),
-        (lane_row >= 64).astype(jnp.float32).astype(jnp.bfloat16),
-    )
+    keep = lane_masks()
 
     def within(g, carry):
         turned = jnp.transpose(col_s[g])
@@ -429,65 +487,27 @@
     base_b = nt_dot(c_wide, mixing, HIGHEST)
     base_c = plain_dot(b_wide, mixing, HIGHEST)
 
-    def turned_rows(c, g):
-        first = states_in[c, g // 4, 2 * lax.rem(g, 4)].astype(jnp.float32)
-        second = states_in[c, g // 4, 2 * lax.rem(g, 4) + 1].astype(jnp.float32)
-        return (
-            jnp.concatenate([first[:8], second[:8]], axis=0).astype(jnp.bfloat16),
-            jnp.concatenate([first[8:], second[8:]], axis=0).astype(jnp.bfloat16),
-        )
-
-    def spread(one, two):
-        blank = jnp.zeros((2 * STATE, HALF), jnp.bfloat16)
-        top = jnp.concatenate([one * keep[0], one * keep[1]], axis=0)
-        bottom = jnp.concatenate([two * keep[0], two * keep[1]], axis=0)
-        return jnp.concatenate(
-            [
-                jnp.concatenate([top, blank], axis=1),
-                jnp.concatenate([blank, bottom], axis=1),
-            ],
-            axis=0,
-        )
-
-    def across(c, pair, carry):
-        cross_b, cross_c = carry
-        groups = (2 * pair, 2 * pair + 1)
-        lanes = [pl.ds(pl.multiple_of(g * LANES + HALF * c, HALF), HALF) for g in groups]
-        state_one, grad_one = turned_rows(c, groups[0])
-        state_two, grad_two = turned_rows(c, groups[1])
-        state = spread(state_one, state_two)
-        grad = spread(grad_one, grad_two)
-        heads = slice(2 * c, 2 * c + 2)
-        ends = jnp.concatenate([to_end_s[g][heads] for g in groups], axis=0)
-        starts = jnp.concatenate([from_start_s[g][heads] for g in groups], axis=0)
-        into = jnp.concatenate([b_wide * ends[k : k + 1, :] for k in range(4)], axis=0)
-        term = plain_dot(jnp.transpose(into).astype(jnp.bfloat16), grad)
-        for k in range(2):
-            gx_ref[0, :, lanes[k]] = (
-                partial_x[:, lanes[k]] + term[:, HALF * k : HALF * k + HALF]
-            ).astype(jnp.bfloat16)
-        x = jnp.concatenate([xv[:, part] for part in lanes], axis=1)
-        dy = jnp.concatenate([dyv[:, part] for part in lanes], axis=1)
-        from_x = nt_dot(grad, x)
-        from_dy = nt_dot(state, dy)
-        for k in range(4):
-            take = slice(STATE * k, STATE * k + STATE)
-            cross_b += from_x[take] * ends[k : k + 1, :]
-            cross_c += from_dy[take] * starts[k : k + 1, :]
-        return cross_b, cross_c
-
+    def store(g, lanes, tile):
+        gx_ref[0, :, lanes] = tile
+
+    refs = (b_wide, xv, dyv, partial_x, to_end_s, from_start_s, store)
     crosses = (base_b, base_c)
-    for c in range(CHUNKS):
+    b_out[...] = b_ref[...]
+    for c in range(CHUNKS - 1):
         row_wait(states_out.at[c], states_in.at[c], 9 + c).wait_recv()
+        states = states_in.at[c]
         crosses = lax.fori_loop(
             0,
             GROUPS // 4,
-            lambda two, carry, c=c: across(c, 2 * two + 1, across(c, 2 * two, carry)),
+            lambda two, carry, c=c, states=states: across(
+                c, 2 * two + 1, across(c, 2 * two, carry, states, *refs), states, *refs
+            ),
             crosses,
         )
-    cross_b, cross_c = crosses
-    gb_ref[0] = cross_b * scale_b
-    gc_ref[0] = cross_c * scale_c
+    cross_b_ref[0], cross_c_ref[0] = crosses
+    final = CHUNKS - 1
+    row_wait(states_out.at[final], states_in.at[final], 9 + final).wait_recv()
+    late_states[...] = states_in[final]
 
     for c in range(CHUNKS):
         row_wait(parts_out.at[c], parts_in.at[c], c).wait_send()
@@ -498,17 +518,69 @@
     column_wait(quad_in, quad_in, 13).wait_send()
 
 
-def store_results(gx_ref, gb_ref, gc_ref, gx_hbm, gb_hbm, gc_hbm, sem):
+def finish(
+    scale_b,
+    scale_c,
+    early_x,
+    cross_b_ref,
+    cross_c_ref,
+    xv,
+    dyv,
+    partial_x,
+    to_end_s,
+    from_start_s,
+    b_ref,
+    states,
+    gx_hbm,
+    gb_hbm,
+    gc_hbm,
+    late_x,
+    gb_v,
+    gc_v,
+    sem,
+):
+    final = CHUNKS - 1
     copies = []
-    for i in range(8):
-        part = pl.ds(32 * i, 32)
+    for g in range(GROUPS):
+        part = pl.ds(g * LANES, HALF * final)
         copies.append(
-            pltpu.make_async_copy(gx_ref.at[0, part], gx_hbm.at[0, part], sem.at[i])
-        )
-    copies.append(pltpu.make_async_copy(gb_ref, gb_hbm, sem.at[8]))
-    copies.append(pltpu.make_async_copy(gc_ref, gc_hbm, sem.at[9]))
+            pltpu.make_async_copy(early_x.at[0, :, part], gx_hbm.at[0, :, part], sem.at[g])
+        )
     for copy in copies:
         copy.start()
+
+    def store(g, lanes, tile):
+        late_x[g] = tile
+
+    b_wide = b_ref[0].astype(jnp.float32)
+    crosses = (cross_b_ref[0], cross_c_ref[0])
+    for pair in range(GROUPS // 2):
+        crosses = across(
+            final,
+            pair,
+            crosses,
+            states,
+            b_wide,
+            xv,
+            dyv,
+            partial_x,
+            to_end_s,
+            from_start_s,
+            store,
+        )
+        for g in (2 * pair, 2 * pair + 1):
+            part = pl.ds(g * LANES + HALF * final, HALF)
+            copy = pltpu.make_async_copy(
+                late_x.at[g], gx_hbm.at[0, :, part], sem.at[GROUPS + g]
+            )
+            copy.start()
+            copies.append(copy)
+    gb_v[0] = crosses[0] * scale_b
+    gc_v[0] = crosses[1] * scale_c
+    for k, (source, target) in enumerate(((gb_v, gb_hbm), (gc_v, gc_hbm))):
+        copy = pltpu.make_async_copy(source, target, sem.at[2 * GROUPS + k])
+        copy.start()
+        copies.append(copy)
     for copy in copies:
         copy.wait()
 
@@ -526,22 +598,30 @@
             jax.ShapeDtypeStruct(b_matrix.shape, f32),
             jax.ShapeDtypeStruct(c_matrix.shape, f32),
         )
+        rows = (SPAN, columns)
+        between = (
+            pltpu.VMEM(inputs.shape, bf16),
+            pltpu.VMEM(b_matrix.shape, f32),
+            pltpu.VMEM(c_matrix.shape, f32),
+            pltpu.VMEM(rows, bf16),
+            pltpu.VMEM(rows, bf16),
+            pltpu.VMEM(rows, f32),
+            pltpu.VMEM((GROUPS, 8, SPAN), f32),
+            pltpu.VMEM((GROUPS, 8, SPAN), f32),
+            pltpu.VMEM(b_matrix.shape, bf16),
+            pltpu.VMEM((ROWS, COLUMNS, 16, HALF), bf16),
+        )
         results = pl.pallas_call(
-            lambda *refs: kernel(scale_b, scale_c, *refs),
-            out_shape=tuple(pltpu.VMEM(shape.shape, shape.dtype) for shape in shapes),
+            kernel,
+            out_shape=between,
             in_specs=[pl.BlockSpec(memory_space=pltpu.SMEM)] + [whole] * 7,
-            out_specs=(vmem, vmem, vmem),
+            out_specs=(vmem,) * len(between),
             scratch_shapes=[
                 pltpu.SMEM((96,), f32),
                 pltpu.VMEM((1, 96, SPAN), f32),
                 pltpu.VMEM((1, 96, SPAN), f32),
                 pltpu.VMEM((1, STATE, SPAN), bf16),
                 pltpu.VMEM((1, STATE, SPAN), bf16),
-                pltpu.VMEM((SPAN, columns), bf16),
-                pltpu.VMEM((SPAN, columns), bf16),
-                pltpu.VMEM((SPAN, columns), f32),
-                pltpu.VMEM((GROUPS, 8, SPAN), f32),
-                pltpu.VMEM((GROUPS, 8, SPAN), f32),
                 pltpu.VMEM((GROUPS, 8, SPAN), f32),
                 pltpu.VMEM((GROUPS, 8, SPAN), f32),
                 pltpu.VMEM((SPAN, SPAN), f32),
@@ -566,7 +646,7 @@
                 pltpu.SemaphoreType.DMA((14,)),
             ],
             compiler_params=pltpu.CompilerParams(
-                collective_id=0, has_side_effects=True, vmem_limit_bytes=48 * 1024 * 1024
+                collective_id=0, has_side_effects=True, vmem_limit_bytes=24 * 1024 * 1024
             ),
         )(
             lengths,
@@ -584,11 +664,17 @@
             )
         )
         return pl.pallas_call(
-            store_results,
+            lambda *refs: finish(scale_b, scale_c, *refs),
             out_shape=shapes,
-            in_specs=[vmem] * 3,
+            in_specs=[vmem] * len(between),
             out_specs=(whole,) * 3,
-            scratch_shapes=[pltpu.SemaphoreType.DMA((10,))],
+            scratch_shapes=[
+                pltpu.VMEM((GROUPS, SPAN, HALF), bf16),
+                pltpu.VMEM(b_matrix.shape, f32),
+                pltpu.VMEM(c_matrix.shape, f32),
+                pltpu.SemaphoreType.DMA((2 * GROUPS + 2,)),
+            ],
+            compiler_params=pltpu.CompilerParams(vmem_limit_bytes=24 * 1024 * 1024),
         )(*(pltpu.with_memory_space_constraint(result, pltpu.VMEM) for result in results))
 
     return jax.shard_map(

time: 34.8 us -> 33.6 us (0.966)
  Pallas kernels: 33.4 us -> 32.2 us
    pallas_call x2, Pallas kernels: 33.4 us -> 32.2 us  [the longest x1 30.3 us: local(): pl.pallas_call(kernel, out_shape=between, in_specs=[pl.BlockSpec(memory_s...]
where the time goes in v5:
time: 33.6 us; the launch traced here: 33.5 us
  Pallas kernels  32.2 us (96%)
  between operations  1.29 us (4%)
    pallas_call x1, Pallas kernels, local(): pl.pallas_call(kernel, out_shape=between, in_specs=[pl.BlockSpec(memory_s...  30.3 us
    pallas_call x1, Pallas kernels, local(): pl.pallas_call(lambda *refs: finish(scale_b, scale_c, *refs), out_shape=s...  1.95 us

profile of v5, /device:TPU:16, one launch (start us, length us, event | category | flops | bytes accessed | tf_op | source)
XLA Modules:
  0.0 33.5 jit_solution(5199767439762494810)
XLA Ops:
  1.3 30.3 %shard_map.103 = (bf16[1,256,6144]{2,1,0:T(8,128)(2,1)S(1)}, f32[1,16,256]{2,1,0:T(8,128)S(1)}, f32[1,16,256]{2,1,0:T(8,128)S(1)}, bf16[256,6144]{1,0:T(8,128)(2...) custom-call(s32[1]{0:T(128)S(6)} %copy.11.length_ref, ...), custom_call_target="tpu_custom_call" | custom-call | tf_op jit(solution)/shard_map/pallas_call | solution.py:614
  31.5 2.0 %shard_map.104 = (bf16[1,256,6144]{2,1,0:T(8,128)(2,1)}, f32[1,16,256]{2,1,0:T(8,128)}, f32[1,16,256]{2,1,0:T(8,128)}) custom-call(bf16[1,256,6144]{2,1,0:T(8,128)(2,1)S(1)} %get-tuple-element.13.refs_0_, f32[1,16,256]{2,1,0:T(8,128)S(1)} %get-tuple-element.14.refs_1_, f32[1,16,256]{2,1,0:T(8,128)S(1)} %get-tuple-element.15.refs_2_, ...), custom_call_target="tpu_custom_call" | custom-call | tf_op jit(solution)/shard_map/pallas_call | solution.py:666

commit v6 on v5

--- a/solution.py
+++ b/solution.py
@@ -22,6 +22,7 @@
 COLUMNS = 8
 CHUNKS = 3
 QUARTER = 1536
+WAIT_AFTER = 1
 FILL = (2, 1, 1, 2, 1, 2, 2, 1, 1, 2, 1)
 NT = (((1,), (1,)), ((), ()))
 
@@ -313,11 +314,13 @@
             ),
             0,
         )
-        if i == 0:
+        if i == WAIT_AFTER:
             pl.semaphore_wait(barrier, ROWS + COLUMNS - 2)
-        if i < ROWS - 1:
-            dx = row_offsets[i]
-            remote(ends_out.at[quarter], ends_in.at[my_x], 12, row_device(dx)).start()
+            ready = row_offsets[: i + 1]
+        else:
+            ready = row_offsets[i : i + 1] if i > WAIT_AFTER else ()
+        for dx in ready:
+            remote(ends_out.at[row_peer(dx)], ends_in.at[my_x], 12, row_device(dx)).start()
             send_part(0, dx)
     send_parts(1)
     for c in range(CHUNKS):

time: 33.6 us -> 33.3 us (level)
    pallas_call x1, Pallas kernels: 30.3 us -> 29.9 us  [local(): pl.pallas_call(kernel, out_shape=between, in_specs=[pl.BlockSpec(memory_s...]
where the time goes in v6:
time: 33.3 us; the launch traced here: 33.2 us
  Pallas kernels  31.9 us (96%)
  between operations  1.29 us (4%)
    pallas_call x1, Pallas kernels, local(): pl.pallas_call(kernel, out_shape=between, in_specs=[pl.BlockSpec(memory_s...  29.9 us
    pallas_call x1, Pallas kernels, local(): pl.pallas_call(lambda *refs: finish(scale_b, scale_c, *refs), out_shape=s...  1.95 us

profile of v6, /device:TPU:16, one launch (start us, length us, event | category | flops | bytes accessed | tf_op | source)
XLA Modules:
  0.0 33.2 jit_solution(17585360811085915491)
XLA Ops:
  1.3 29.9 %shard_map.103 = (bf16[1,256,6144]{2,1,0:T(8,128)(2,1)S(1)}, f32[1,16,256]{2,1,0:T(8,128)S(1)}, f32[1,16,256]{2,1,0:T(8,128)S(1)}, bf16[256,6144]{1,0:T(8,128)(2...) custom-call(s32[1]{0:T(128)S(6)} %copy.11.length_ref, ...), custom_call_target="tpu_custom_call" | custom-call | tf_op jit(solution)/shard_map/pallas_call | solution.py:617
  31.2 2.0 %shard_map.104 = (bf16[1,256,6144]{2,1,0:T(8,128)(2,1)}, f32[1,16,256]{2,1,0:T(8,128)}, f32[1,16,256]{2,1,0:T(8,128)}) custom-call(bf16[1,256,6144]{2,1,0:T(8,128)(2,1)S(1)} %get-tuple-element.13.refs_0_, f32[1,16,256]{2,1,0:T(8,128)S(1)} %get-tuple-element.14.refs_1_, f32[1,16,256]{2,1,0:T(8,128)S(1)} %get-tuple-element.15.refs_2_, ...), custom_call_target="tpu_custom_call" | custom-call | tf_op jit(solution)/shard_map/pallas_call | solution.py:669
